TPU v7x, 32 devices: a whole 2x2x4 slice. The times are simulated.
32 devices in a mesh: gx: 4 (over z), gy: 4 (over y, x), gz: 2 (over core).
Axes of the slice: x: 2, y: 2, z: 4, core: 2. Of those that a mesh axis runs over, the one named last changes fastest.
Arguments:
- source_points: float32 [3, 13, 4, 16, 4, 512], P(None, None, 'gx', 'gy', 'gz'), may hold values from -3 to 3
- target_points: float32 [3, 13, 4, 16, 4, 512], P(None, None, 'gx', 'gy', 'gz'), may hold values from -3 to 3
- normals: float32 [3, 13, 4, 16, 4, 512], P(None, None, 'gx', 'gy', 'gz'), may hold values from -4 to 4
- weights: float32 [13, 4, 16, 4, 512], P(None, 'gx', 'gy', 'gz'), may hold values from 0.1 to 1
- blocks: int32 [13, 4, 16, 4], P(None, 'gx', 'gy', 'gz'), may hold values from 0 to 2
- affines: float32 [12, 4, 16, 4], P(None, 'gx', 'gy', 'gz'), may hold values from -0.5 to 0.5
- anchor: int32 [1], replicated, may hold values from 0 to 255
Outputs:
- update: float32 [12, 4, 16, 4], P(None, 'gx', 'gy', 'gz')
- residual: float32 [12, 4, 16, 4], P(None, 'gx', 'gy', 'gz')
Inputs may be any that keep to these rules, and one draw needn't show every extreme that they name: `blocks`: number of 256-point correspondence blocks of the correlation; entries of correlations whose second tile lies outside the grid are not read. `anchor`: a tile index (x 16 + y) * 4 + z.
All inputs are finite; a program needn't handle non-finite values.
Results may differ from a plain program's by a relative error of at most 0.0003.
Values sent between devices are 32-bit elements; how exact they have to be, the bound alone decides.
A program may use at most 128 MiB of HBM per device.

v0:
```python
import functools

import jax
import jax.numpy as jnp
import numpy as np
from jax import lax
from jax.experimental import pallas as pl
from jax.experimental.pallas import tpu as pltpu
from jax.sharding import PartitionSpec as P

BLOCK = 256
ITERS = 10
SPACING = 0.5
DAMPING = 1.0
OFFSETS = (
    (1, 0, 0),
    (0, 1, 0),
    (0, 0, 1),
    (1, 1, -1),
    (1, -1, 1),
    (-1, 1, 1),
    (1, 1, 0),
    (1, 0, 1),
    (0, 1, 1),
    (1, 1, 1),
    (1, -1, 0),
    (0, 1, -1),
    (-1, 0, 1),
)
DIRS = len(OFFSETS)
SLOTS = 16
PAIR_ROWS = 96
BACK_ROWS = 64
ROWS = PAIR_ROWS + BACK_ROWS
AXES = ("gx", "gy", "gz")
MESH = pl.DeviceIdType.MESH
VMEM_BYTES = 60 * 1024 * 1024

NORMAL_PAIRS = [(c, k) for c in range(3) for k in range(c, 3)]
POINT_PAIRS = [(e, k) for e in range(4) for k in range(e, 4)]


def normal_pair(c, k):
    return NORMAL_PAIRS.index((min(c, k), max(c, k)))


def point_pair(e, k):
    return POINT_PAIRS.index((min(e, k), max(e, k)))


def grouped(count, group, body):
    def trip(i, carry):
        for j in range(group):
            body(i * group + j)
        return carry

    whole = count // group
    lax.fori_loop(0, whole, trip, 0)
    for i in range(whole * group, count):
        body(i)


def moved_targets(target):
    views = {d: target[:, d] for d in range(DIRS)}
    for axis, name in enumerate(AXES):
        dim = 1 + axis
        devices = lax.axis_size(name)
        for sign in (1, -1):
            members = [d for d in range(DIRS) if OFFSETS[d][axis] == sign]
            if not members:
                continue
            length = views[members[0]].shape[dim]
            edge = 0 if sign > 0 else length - 1
            slab = jnp.stack(
                [lax.slice_in_dim(views[d], edge, edge + 1, axis=dim) for d in members]
            )
            if sign > 0:
                links = [(i + 1, i) for i in range(devices - 1)]
            else:
                links = [(i, i + 1) for i in range(devices - 1)]
            came = lax.ppermute(slab, name, links)
            for place, d in enumerate(members):
                if sign > 0:
                    kept = lax.slice_in_dim(views[d], 1, length, axis=dim)
                    pieces = [kept, came[place]]
                else:
                    kept = lax.slice_in_dim(views[d], 0, length - 1, axis=dim)
                    pieces = [came[place], kept]
                views[d] = jnp.concatenate(pieces, axis=dim)
    return jnp.stack([views[d] for d in range(DIRS)], axis=1)


def assemble_kernel(tiles, source, target, normal, weight, lane_table, affine, out, turned, acc):
    width = SLOTS * tiles
    points = source.shape[2]
    filling = jnp.zeros((width - DIRS * tiles, 128), jnp.float32)

    def turn(block):
        return jnp.concatenate([block, filling], axis=0).T

    for start in range(0, points, 128):
        spots = pl.ds(start, 128)
        for c in range(3):
            turned[c, spots, :] = turn(source[c, :, spots])
            turned[3 + c, spots, :] = turn(target[c, :, spots])
            turned[6 + c, spots, :] = turn(normal[c, :, spots])
        turned[9, spots, :] = turn(weight[:, spots])
    acc[...] = jnp.zeros_like(acc)
    step = 32
    limit = lane_table[3:4, :]

    def body(chunk, carry):
        base = pl.multiple_of(chunk * step, step)
        spots = pl.ds(base, step)
        p = [turned[c, spots, :] for c in range(3)] + [None]
        q = [turned[3 + c, spots, :] for c in range(3)] + [None]
        n = [turned[6 + c, spots, :] for c in range(3)]
        index = base + lax.broadcasted_iota(jnp.int32, (step, width), 0)
        w = jnp.where(index.astype(jnp.float32) < limit, turned[9, spots, :], 0.0)

        def times(left, right):
            if left is None:
                return right
            return left if right is None else left * right

        def add(row, value):
            acc[row] += jnp.sum(value.reshape(step // 8, 8, width), axis=0)

        weighted = [w * n[c] * n[k] for c, k in NORMAL_PAIRS]
        for e in range(4):
            for k in range(4):
                product = times(p[e], q[k])
                for s in range(6):
                    add(s * 16 + e * 4 + k, times(weighted[s], product))
        for first, here in ((PAIR_ROWS, q), (ROWS, p)):
            for place, (e, k) in enumerate(POINT_PAIRS):
                product = times(here[e], here[k])
                for s in range(6):
                    add(first + s * 10 + place, times(weighted[s], product))
        return carry

    lax.fori_loop(0, points // step, body, 0)

    lane = lax.broadcasted_iota(jnp.int32, (8, width), 1)
    in_pairs = lane < DIRS * tiles

    def all_slots(value):
        for span in (8, 4, 2, 1):
            value = value + pltpu.roll(value, span * tiles, 1)
        return value

    here_rows = [jnp.sum(acc[ROWS + r : ROWS + r + 8], axis=1) for r in range(0, BACK_ROWS, 8)]
    stride = []
    for c in range(3):
        for e in range(4):
            total = 0.0
            for k in range(3):
                row = normal_pair(c, k) * 10 + point_pair(e, 3)
                total = total + here_rows[row // 8][row % 8 : row % 8 + 1] * lane_table[k : k + 1, :]
            stride.append(total)
    stride += [jnp.zeros((1, width), jnp.float32)] * 4
    last_slot = lane >= (SLOTS - 1) * tiles
    for r in range(0, PAIR_ROWS, 8):
        rows = jnp.sum(acc[r : r + 8], axis=1)
        if r < 16:
            rows = rows + affine[r : r + 8, :]
            rows = jnp.where(last_slot, all_slots(jnp.concatenate(stride[r : r + 8], axis=0)), rows)
        out[r : r + 8, :] = rows
    for r in range(0, BACK_ROWS, 8):
        there = jnp.sum(acc[PAIR_ROWS + r : PAIR_ROWS + r + 8], axis=1)
        out[PAIR_ROWS + r : PAIR_ROWS + r + 8, :] = jnp.where(
            in_pairs, there, all_slots(here_rows[r // 8])
        )


def gather_kernel(sizes, mine, out, local_sem, send_sem, recv_sem, hand_sem, take_sem):
    count_x, count_y, count_z = sizes
    chips_z = count_z // 2
    chips = count_x * count_y * chips_z
    at_x, at_y, at_z = (lax.axis_index(name) for name in AXES)
    core = at_z % 2
    chip = (at_x * count_y + at_y) * chips_z + at_z // 2

    def place(which, on_core):
        z = (which % chips_z) * 2 + on_core
        rest = which // chips_z
        return rest // count_y, rest % count_y, z

    def slot(which, on_core):
        x, y, z = place(which, on_core)
        return (x * count_y + y) * count_z + z

    barrier = pltpu.get_barrier_semaphore()
    sibling = place(chip, 1 - core)

    def greet(k, carry):
        other = place((chip + k) % chips, core)
        pl.semaphore_signal(barrier, inc=1, device_id=other, device_id_type=MESH)
        return carry

    lax.fori_loop(1, chips, greet, 0)
    pl.semaphore_signal(barrier, inc=1, device_id=sibling, device_id_type=MESH)
    pl.semaphore_wait(barrier, chips)

    me = slot(chip, core)
    own = pltpu.make_async_copy(mine, out.at[me], local_sem)
    own.start()

    def outgoing(k):
        return pltpu.make_async_remote_copy(
            src_ref=mine,
            dst_ref=out.at[me],
            send_sem=send_sem.at[k],
            recv_sem=recv_sem.at[k],
            device_id=place((chip + k) % chips, core),
            device_id_type=MESH,
        )

    def handed(k):
        origin = slot((chip + chips - k) % chips, core)
        return pltpu.make_async_remote_copy(
            src_ref=out.at[origin],
            dst_ref=out.at[origin],
            send_sem=hand_sem.at[k],
            recv_sem=take_sem.at[k],
            device_id=sibling,
            device_id_type=MESH,
        )

    def first_hand():
        return pltpu.make_async_remote_copy(
            src_ref=mine,
            dst_ref=out.at[me],
            send_sem=hand_sem.at[0],
            recv_sem=take_sem.at[0],
            device_id=sibling,
            device_id_type=MESH,
        )

    def send(k, carry):
        outgoing(k).start()
        return carry

    def forward(k, carry):
        outgoing(k).wait_recv()
        handed(k).start()
        return carry

    def finish(k, carry):
        outgoing(k).wait_send()
        handed(k).wait()
        return carry

    first_hand().start()
    lax.fori_loop(1, chips, send, 0)
    lax.fori_loop(1, chips, forward, 0)
    first_hand().wait()
    lax.fori_loop(1, chips, finish, 0)
    own.wait()


def turn_kernel(tiles, gathered, out):
    width = gathered.shape[2]

    def body(chunk):
        rows = pl.ds(pl.multiple_of(chunk * 8, 8), 8)
        slot = lax.broadcasted_iota(jnp.int32, (8, width), 1) // tiles
        values = [gathered[j, rows, :] for j in range(SLOTS)]
        for span in (1, 2, 4, 8):
            low = (slot & span) == 0
            fresh = list(values)
            for j in range(SLOTS):
                if j & span:
                    continue
                first, second = values[j], values[j + span]
                fresh[j] = jnp.where(low, first, pltpu.roll(second, span * tiles, 1))
                fresh[j + span] = jnp.where(
                    low, pltpu.roll(first, width - span * tiles, 1), second
                )
            values = fresh
        for j in range(SLOTS):
            out[j, rows, :] = values[j]

    grouped(ROWS // 8, 5, body)


def solve_kernel(
    bricks, devices, anchor, parts, table, update_out, residual_out, blocks, inverse, ahead, sent, image
):
    span = parts.shape[2]
    tiles = bricks[0] * bricks[1] * bricks[2]
    group = DIRS if span <= 512 else 1
    inner = (bricks[1] * bricks[2], bricks[2], 1)
    outer = (devices[1] * devices[2] * tiles, devices[2] * tiles, tiles)

    def pull(value, axis, sign):
        near = (sign * inner[axis]) % span
        far = (sign * (outer[axis] - (bricks[axis] - 1) * inner[axis])) % span
        row = axis * 4 + (0 if sign > 0 else 2)
        result = pltpu.roll(value, (span - far) % span, 1) * table[row + 1 : row + 2, :]
        if bricks[axis] > 1:
            result = result + pltpu.roll(value, (span - near) % span, 1) * table[row : row + 1, :]
        return result

    def all_ahead(value):
        result = []
        by_z = {0: value}
        by_yz = {}
        for dx, dy, dz in OFFSETS:
            if dz not in by_z:
                by_z[dz] = pull(value, 2, dz)
            if (dy, dz) not in by_yz:
                by_yz[dy, dz] = pull(by_z[dz], 1, dy) if dy else by_z[dz]
            result.append(pull(by_yz[dy, dz], 0, dx) if dx else by_yz[dy, dz])
        return result

    def fold(read):
        by_yz = {}
        for d, (dx, dy, dz) in enumerate(OFFSETS):
            term = read(d)
            term = pull(term, 0, -dx) if dx else term
            by_yz[dy, dz] = by_yz[dy, dz] + term if (dy, dz) in by_yz else term
        by_z = {}
        for (dy, dz), term in by_yz.items():
            term = pull(term, 1, -dy) if dy else term
            by_z[dz] = by_z[dz] + term if dz in by_z else term
        total = None
        for dz, term in by_z.items():
            term = pull(term, 2, -dz) if dz else term
            total = term if total is None else total + term
        return total

    def operate(vector, shifted):
        for d, value in enumerate(all_ahead(vector)):
            ahead[d] = value
        ahead[DIRS] = vector

        def forward(a):
            total = blocks[0, a] * ahead[0]
            for d in range(1, DIRS + 1):
                total = total + blocks[d, a] * ahead[d]
            image[pl.ds(a, 1), :] = jnp.sum(total, axis=0, keepdims=True)

        grouped(12, min(group, 12), forward)
        if shifted is None:

            def backward(d):
                total = blocks[d, 0] * vector[0:1]
                for a in range(1, 12):
                    total = total + blocks[d, a] * vector[a : a + 1]
                sent[d] = total

            grouped(DIRS, group, backward)
        else:
            for d in range(DIRS):
                total = None
                for a in range(12):
                    scale = vector[a : a + 1]
                    if a % 4 == 3 and OFFSETS[d][a // 4]:
                        scale = scale - SPACING * OFFSETS[d][a // 4]
                    term = blocks[d, a] * scale
                    total = term if total is None else total + term
                sent[d] = total
        return image[...] + fold(lambda d: sent[d])

    image[...] = jnp.zeros_like(image)
    no_rows = jnp.zeros((4, span), jnp.float32)

    def expand(d, carry):
        for c in range(3):
            for e in range(4):
                for k in range(3):
                    first = normal_pair(c, k) * 16 + e * 4
                    blocks[d, 4 * c + e, 4 * k : 4 * k + 4, :] = -parts[d, first : first + 4, :]
                blocks[d, 4 * c + e, 12:16, :] = no_rows
        return carry

    lax.fori_loop(0, DIRS, expand, 0)
    diag = parts[DIRS, PAIR_ROWS:ROWS, :] + fold(lambda d: parts[d, PAIR_ROWS:ROWS, :])
    for c in range(3):
        for e in range(4):
            for k in range(3):
                for f in range(4):
                    row = normal_pair(c, k) * 10 + point_pair(e, f)
                    blocks[DIRS, 4 * c + e, 4 * k + f : 4 * k + f + 1, :] = diag[row : row + 1]
            blocks[DIRS, 4 * c + e, 12:16, :] = no_rows

    rank = lax.broadcasted_iota(jnp.int32, (16, span), 0)
    unit = ((rank == 0) | (rank == 5) | (rank == 10)).astype(jnp.float32)
    keep = (table[12:13, :] != anchor[0].astype(jnp.float32)).astype(jnp.float32)
    matrix = parts[DIRS + 1, 0:16, :] + unit
    grad = operate(matrix, True) - SPACING * parts[DIRS + 2, 0:16, :]
    rhs = -(keep * grad)

    keep_all = jnp.broadcast_to(keep, (8, span))
    for d, value in enumerate(all_ahead(keep_all)):
        both = keep * value[0:1]

        def mask(a, carry, d=d, both=both):
            blocks[d, a] = blocks[d, a] * both
            return carry

        lax.fori_loop(0, 12, mask, 0)
    rows = []
    for a in range(12):
        eye = (rank == a).astype(jnp.float32)
        row = keep * (blocks[DIRS, a] + DAMPING * eye) + (1.0 - keep) * eye
        blocks[DIRS, a] = row
        inverse[a] = row
    for pivot in range(12):
        here = inverse[pivot]
        factor = 1.0 / here[pivot : pivot + 1]
        at_pivot = rank == pivot
        scaled_row = jnp.where(at_pivot, factor, here * factor)
        for a in range(12):
            if a == pivot:
                inverse[a] = scaled_row
            else:
                row = inverse[a]
                column = row[pivot : pivot + 1]
                inverse[a] = jnp.where(at_pivot, 0.0, row) - column * scaled_row

    def precondition(vector):
        parts_of = [jnp.sum(inverse[a] * vector, axis=0, keepdims=True) for a in range(12)]
        return jnp.concatenate(parts_of + [no_rows], axis=0)

    def dot(left, right):
        return jnp.sum(left * right, keepdims=True)

    first = precondition(rhs)

    def step(_, carry):
        update, residual, direction, inner_now = carry
        along = operate(direction, None)
        alpha = inner_now / dot(direction, along)
        update = update + alpha * direction
        residual = residual - alpha * along
        scaled = precondition(residual)
        inner_next = dot(residual, scaled)
        direction = scaled + (inner_next / inner_now) * direction
        return update, residual, direction, inner_next

    start = (jnp.zeros_like(rhs), rhs, first, dot(rhs, first))
    update, residual, _, _ = lax.fori_loop(0, ITERS, step, start)
    update_out[...] = update
    residual_out[...] = residual


def lane_masks(bricks, devices):
    shape = tuple(devices) + tuple(bricks)
    index = np.indices(shape).reshape(6, -1)
    table = np.zeros((16, index.shape[1]), np.float32)
    flat = 0
    for axis in range(3):
        outer, inner = index[axis], index[3 + axis]
        end = inner == bricks[axis] - 1
        table[4 * axis] = ~end
        table[4 * axis + 1] = end & (outer < devices[axis] - 1)
        table[4 * axis + 2] = inner > 0
        table[4 * axis + 3] = (inner == 0) & (outer > 0)
        flat = flat * (devices[axis] * bricks[axis]) + outer * bricks[axis] + inner
    table[12] = flat
    return table


def on_device(source_points, target_points, normals, weights, blocks, affines, anchor):
    bricks = source_points.shape[2:5]
    points = source_points.shape[5]
    devices = tuple(lax.axis_size(name) for name in AXES)
    count = devices[0] * devices[1] * devices[2]
    tiles = bricks[0] * bricks[1] * bricks[2]
    width = SLOTS * tiles
    span = count * tiles
    params = functools.partial(pltpu.CompilerParams, vmem_limit_bytes=VMEM_BYTES)
    vmem = pl.BlockSpec(memory_space=pltpu.VMEM)

    inside = jnp.ones((DIRS,) + bricks, jnp.float32)
    for axis, name in enumerate(AXES):
        spots = lax.axis_index(name) * bricks[axis] + np.arange(bricks[axis], dtype=np.int32)
        total = devices[axis] * bricks[axis]
        steps = np.array([offset[axis] for offset in OFFSETS], np.int32).reshape(-1, 1)
        ahead = spots.reshape(1, -1) + steps
        fits = ((ahead >= 0) & (ahead < total)).astype(jnp.float32)
        inside = inside * fits.reshape((DIRS,) + tuple(-1 if i == axis else 1 for i in range(3)))
    limit = (BLOCK * blocks.astype(jnp.float32) * inside).reshape(1, DIRS * tiles)
    strides = np.repeat(np.array(OFFSETS, np.float32).T, tiles, axis=1)
    lane_table = jnp.concatenate(
        [jnp.asarray(strides), limit, jnp.zeros((4, DIRS * tiles), jnp.float32)]
    )
    lane_table = jnp.pad(lane_table, ((0, 0), (0, width - DIRS * tiles)))
    affine = jnp.pad(
        affines.reshape(12, tiles), ((0, 4), ((DIRS + 1) * tiles, width - (DIRS + 2) * tiles))
    )

    def flat(value):
        lead = value.shape[:-5]
        return value.reshape(lead + (DIRS * tiles, points))

    local = pl.pallas_call(
        functools.partial(assemble_kernel, tiles),
        out_shape=jax.ShapeDtypeStruct((ROWS, width), jnp.float32),
        in_specs=[vmem] * 6,
        out_specs=vmem,
        scratch_shapes=[
            pltpu.VMEM((10, points, width), jnp.float32),
            pltpu.VMEM((ROWS + BACK_ROWS, 8, width), jnp.float32),
        ],
        compiler_params=params(),
        name="assemble",
    )(
        flat(source_points),
        flat(moved_targets(target_points)),
        flat(normals),
        flat(weights),
        lane_table,
        affine,
    )
    chips = count // 2
    gathered = pl.pallas_call(
        functools.partial(gather_kernel, devices),
        out_shape=jax.ShapeDtypeStruct((count, ROWS, width), jnp.float32),
        in_specs=[vmem],
        out_specs=pl.BlockSpec(memory_space=pl.ANY),
        scratch_shapes=[pltpu.SemaphoreType.DMA] + [pltpu.SemaphoreType.DMA((chips,))] * 4,
        compiler_params=params(collective_id=0, has_side_effects=True),
        name="gather",
    )(local)
    parts = pl.pallas_call(
        functools.partial(turn_kernel, tiles),
        grid=(count // SLOTS,),
        out_shape=jax.ShapeDtypeStruct((SLOTS, ROWS, span), jnp.float32),
        in_specs=[pl.BlockSpec((SLOTS, ROWS, width), lambda g: (g, 0, 0))],
        out_specs=pl.BlockSpec((SLOTS, ROWS, width), lambda g: (0, 0, g)),
        compiler_params=params(),
        name="turn",
    )(gathered)
    update, residual = pl.pallas_call(
        functools.partial(solve_kernel, bricks, devices),
        out_shape=[jax.ShapeDtypeStruct((16, span), jnp.float32)] * 2,
        in_specs=[pl.BlockSpec(memory_space=pltpu.SMEM), vmem, vmem],
        out_specs=[vmem, vmem],
        scratch_shapes=[
            pltpu.VMEM((DIRS + 1, 12, 16, span), jnp.float32),
            pltpu.VMEM((12, 16, span), jnp.float32),
            pltpu.VMEM((DIRS + 1, 16, span), jnp.float32),
            pltpu.VMEM((DIRS, 16, span), jnp.float32),
            pltpu.VMEM((16, span), jnp.float32),
        ],
        compiler_params=params(),
        name="solve",
    )(anchor, parts, jnp.asarray(lane_masks(bricks, devices)))
    me = (lax.axis_index("gx") * devices[1] + lax.axis_index("gy")) * devices[2]
    me = me + lax.axis_index("gz")

    def mine(value):
        return lax.dynamic_slice(value, (0, me * tiles), (12, tiles)).reshape((12,) + bricks)

    return mine(update), mine(residual)


def solution(mesh):
    placed = (
        P(None, None, "gx", "gy", "gz", None),
        P(None, None, "gx", "gy", "gz", None),
        P(None, None, "gx", "gy", "gz", None),
        P(None, "gx", "gy", "gz", None),
        P(None, "gx", "gy", "gz"),
        P(None, "gx", "gy", "gz"),
        P(),
    )
    return jax.shard_map(
        on_device,
        mesh=mesh,
        in_specs=placed,
        out_specs=(P(None, "gx", "gy", "gz"), P(None, "gx", "gy", "gz")),
        check_vma=False,
    )
```

profile of v0, /device:TPU:15, one launch (start us, length us, event | category | flops | bytes accessed | tf_op | source)
XLA Modules:
  0.0 103.4 jit_solution(17146380054341921356)
XLA Ops:
  0.7 1.4 %fusion.21 = (f32[3,1,1,4,2,512]{5,4,3,2,1,0:T(2,128)S(1)}, f32[3,1,1,4,2,512]{5,4,3,2,1,0:T(2,128)S(1)}, f32[3,1,1,4,2,512]{5,4,3,2,1,0:T(2,128)S(1)}, f32[3,1,...) fusion(f32[3,13,1,4,2,512]{5,4,3,2,1,0:T(2,128)} %param.16), kind=kLoop, calls=%fused_computation.143 | loop fusion | bytes 1277952 | tf_op jit(solution)/shard_map/slice | solution.py:64
  2.2 3.2 %collective-permute-start.1 = (f32[2,3,1,4,2,512]{5,4,1,3,2,0:T(2,128)S(1)}, f32[2,3,1,4,2,512]{5,4,1,3,2,0:T(2,128)S(1)}, u32[]{:S(2)}, u32[]{:S(2)}) collective-permute-start(f32[2,3,1,4,2,512]{5,4,1,3,2,0:T(2,128)S(1)} %pad_maximum_fusion), channel_id=1, source_target_pairs={{0,8},{8,16},{16,24},{1,9},{9,17},{17,25},{2,10},{10,18},{18,26},{... | collective-permute-start | bytes 294920 | tf_op jit(solution)/shard_map/ppermute | solution.py:81
  5.5 2.1 %collective-permute-start = (f32[7,3,1,4,2,512]{5,4,1,3,2,0:T(2,128)S(1)}, f32[7,3,1,4,2,512]{5,4,1,3,2,0:T(2,128)S(1)}, u32[]{:S(2)}, u32[]{:S(2)}) collective-permute-start(f32[7,3,1,4,2,512]{5,4,1,3,2,0:T(2,128)S(1)} %constant_dynamic-update-slice_fusion), channel_id=1, source_target_pairs={{8,0},{16,8},{24,16},{9,1},{17,9},{25,17},{10,2},{18,10},{26,18},{... | collective-permute-start | bytes 1032200 | tf_op jit(solution)/shard_map/ppermute | solution.py:81
  8.3 0.7 and_convert_fusion
  9.0 0.7 fusion.19
  9.8 0.7 multiply_multiply_fusion
  11.7 0.7 pad.9.affine
  13.0 0.8 reshape.115.weight
  13.8 1.3 %reshape.112.source = f32[3,104,512]{2,1,0:T(8,128)} reshape(f32[3,13,1,4,2,512]{5,4,3,2,1,0:T(2,128)S(1)} %copy-done) | data formatting | bytes 1277952 | tf_op jit(solution)/shard_map/reshape | solution.py:497
  15.1 1.3 %reshape.114.normal = f32[3,104,512]{2,1,0:T(8,128)} reshape(f32[3,13,1,4,2,512]{5,4,3,2,1,0:T(2,128)S(1)} %copy-done.1) | data formatting | bytes 1277952 | tf_op jit(solution)/shard_map/reshape | solution.py:497
  16.7 1.3 %collective-permute-start.3 = (f32[2,3,1,1,2,512]{5,4,1,3,2,0:T(2,128)S(1)}, f32[2,3,1,1,2,512]{5,4,1,3,2,0:T(2,128)S(1)}, u32[]{:S(2)}, u32[]{:S(2)}) collective-permute-start(f32[2,3,1,1,2,512]{5,4,1,3,2,0:T(2,128)S(1)} %pad_maximum_fusion.8), channel_id=1, source_target_pairs={{0,2},{2,4},{4,6},{1,3},{3,5},{5,7},{8,10},{10,12},{12,14},{9,11},... | collective-permute-start | bytes 73736 | tf_op jit(solution)/shard_map/ppermute | solution.py:81
  18.1 4.0 %collective-permute-start.2 = (f32[7,3,1,1,2,512]{5,4,1,3,2,0:T(2,128)S(1)}, f32[7,3,1,1,2,512]{5,4,1,3,2,0:T(2,128)S(1)}, u32[]{:S(2)}, u32[]{:S(2)}) collective-permute-start(f32[7,3,1,1,2,512]{5,4,1,3,2,0:T(2,128)S(1)} %constant_dynamic-update-slice_fusion.7), channel_id=1, source_target_pairs={{2,0},{4,2},{6,4},{3,1},{5,3},{7,5},{10,8},{12,10},{14,12},{11,9},... | collective-permute-start | bytes 258056 | tf_op jit(solution)/shard_map/ppermute | solution.py:81
  22.2 1.4 %collective-permute-done.2 = f32[7,3,1,1,2,512]{5,4,1,3,2,0:T(2,128)S(1)} collective-permute-done((f32[7,3,1,1,2,512]{5,4,1,3,2,0:T(2,128)S(1)}, f32[7,3,1,1,2,512]{5,4,1,3,2,0:T(2,128)S(1)}, u32[]{:S(2)}, u32[]{:S(2)}) %collective-permute-start.2) | collective-permute-done | bytes 86048 | tf_op jit(solution)/shard_map/ppermute | solution.py:81
  23.7 1.3 %collective-permute-start.5 = (f32[2,3,1,4,1,512]{5,3,1,4,2,0:T(4,128)S(1)}, f32[2,3,1,4,1,512]{5,3,1,4,2,0:T(4,128)S(1)}, u32[]{:S(2)}, u32[]{:S(2)}) collective-permute-start(f32[2,3,1,4,1,512]{5,3,1,4,2,0:T(4,128)S(1)} %pad_maximum_fusion.7), channel_id=1, source_target_pairs={{0,1},{2,3},{4,5},{6,7},{8,9},{10,11},{12,13},{14,15},{16,17},{18,... | collective-permute-start | bytes 147464 | tf_op jit(solution)/shard_map/ppermute | solution.py:81
  25.2 4.4 %collective-permute-start.4 = (f32[7,3,1,4,1,512]{5,3,1,4,2,0:T(4,128)S(1)}, f32[7,3,1,4,1,512]{5,3,1,4,2,0:T(4,128)S(1)}, u32[]{:S(2)}, u32[]{:S(2)}) collective-permute-start(f32[7,3,1,4,1,512]{5,3,1,4,2,0:T(4,128)S(1)} %constant_dynamic-update-slice_fusion.14), channel_id=1, source_target_pairs={{1,0},{3,2},{5,4},{7,6},{9,8},{11,10},{13,12},{15,14},{17,16},{19,... | collective-permute-start | bytes 516104 | tf_op jit(solution)/shard_map/ppermute | solution.py:81
  29.8 0.9 collective-permute-done.4
  32.0 1.3 %reshape.113.target = f32[3,104,512]{2,1,0:T(8,128)} reshape(f32[3,13,1,4,2,512]{5,4,3,1,0,2:T(2,128)S(1)} %copy.815) | data formatting | bytes 1277952 | tf_op jit(solution)/shard_map/reshape | solution.py:497
  33.2 6.7 %assemble.1.mine = f32[160,128]{1,0:T(8,128)} custom-call(f32[3,104,512]{2,1,0:T(8,128)} %reshape.112.source, f32[3,104,512]{2,1,0:T(8,128)} %reshape.113.target, f32[3,104,512]{2,1,0:T(8,128)} %reshape.114.normal, f32[104,512]{1,0:T(8,128)} %reshape.115.weight, f32[8,128]{1,0:T(8,128)} %pad.8.lane_table, f32[16,128]{1,0:T(8,128)} %pad.9.affine), custom_call_target="tpu_custom_call" | custom-call | tf_op jit(solution)/shard_map/assemble/pallas_call | solution.py:499
  39.9 39.8 %gather.1.gathered = f32[32,160,128]{2,1,0:T(8,128)} custom-call(f32[160,128]{1,0:T(8,128)} %assemble.1.mine), custom_call_target="tpu_custom_call" | custom-call | tf_op jit(solution)/shard_map/gather/pallas_call | solution.py:519
  79.7 7.6 %turn.1.parts = f32[16,160,256]{2,1,0:T(8,128)} custom-call(f32[32,160,128]{2,1,0:T(8,128)} %gather.1.gathered), custom_call_target="tpu_custom_call" | custom-call | tf_op jit(solution)/shard_map/turn/pallas_call | solution.py:528
  87.3 13.2 %solve.1 = (f32[16,256]{1,0:T(8,128)}, f32[16,256]{1,0:T(8,128)}) custom-call(s32[1]{0:T(128)S(6)} %copy.903.anchor, f32[16,160,256]{2,1,0:T(8,128)} %turn.1.parts, f32[16,256]{1,0:T(8,128)} %constant.54.clone.table), custom_call_target="tpu_custom_call" | custom-call | tf_op jit(solution)/shard_map/solve/pallas_call | solution.py:537
  100.5 0.8 constant_dynamic-slice_fusion.1
  101.3 0.8 constant_dynamic-slice_fusion
  102.1 0.7 copy.819
  (103 shorter events, 4.5 us)
Async XLA Ops:
  0.6 10.3 %copy-start.4 = (f32[3,104]{1,0:T(4,128)S(1)}, f32[3,104]{1,0:T(4,128)}, u32[]{:S(2)}) copy-start(f32[3,104]{1,0:T(4,128)} %constant.53.clone) | copy-start | bytes 3748
  0.6 11.0 %copy-start.3 = (f32[12,1,4,2]{0,3,2,1:T(2,128)S(1)}, f32[12,1,4,2]{0,3,2,1:T(2,128)}, u32[]{:S(2)}) copy-start(f32[12,1,4,2]{0,3,2,1:T(2,128)} %param.20) | copy-start | bytes 1156
  0.7 12.3 %copy-start.2 = (f32[13,1,4,2,512]{4,3,2,1,0:T(2,128)S(1)}, f32[13,1,4,2,512]{4,3,2,1,0:T(2,128)}, u32[]{:S(2)}) copy-start(f32[13,1,4,2,512]{4,3,2,1,0:T(2,128)} %param.18) | copy-start | bytes 638980
  0.7 13.2 %copy-start = (f32[3,13,1,4,2,512]{5,4,3,2,1,0:T(2,128)S(1)}, f32[3,13,1,4,2,512]{5,4,3,2,1,0:T(2,128)}, u32[]{:S(2)}) copy-start(f32[3,13,1,4,2,512]{5,4,3,2,1,0:T(2,128)} %param.15) | copy-start | bytes 1916932
  0.7 14.4 %copy-start.1 = (f32[3,13,1,4,2,512]{5,4,3,2,1,0:T(2,128)S(1)}, f32[3,13,1,4,2,512]{5,4,3,2,1,0:T(2,128)}, u32[]{:S(2)}) copy-start(f32[3,13,1,4,2,512]{5,4,3,2,1,0:T(2,128)} %param.17) | copy-start | bytes 1916932
  2.2 14.2 %collective-permute-start.1 = (f32[2,3,1,4,2,512]{5,4,1,3,2,0:T(2,128)S(1)}, f32[2,3,1,4,2,512]{5,4,1,3,2,0:T(2,128)S(1)}, u32[]{:S(2)}, u32[]{:S(2)}) collective-permute-start(f32[2,3,1,4,2,512]{5,4,1,3,2,0:T(2,128)S(1)} %pad_maximum_fusion), channel_id=1, source_target_pairs={{0,8},{8,16},{16,24},{1,9},{9,17},{17,25},{2,10},{10,18},{18,26},{... | collective-permute-start | bytes 294920 | tf_op jit(solution)/shard_map/ppermute | solution.py:81
  5.5 11.0 %collective-permute-start = (f32[7,3,1,4,2,512]{5,4,1,3,2,0:T(2,128)S(1)}, f32[7,3,1,4,2,512]{5,4,1,3,2,0:T(2,128)S(1)}, u32[]{:S(2)}, u32[]{:S(2)}) collective-permute-start(f32[7,3,1,4,2,512]{5,4,1,3,2,0:T(2,128)S(1)} %constant_dynamic-update-slice_fusion), channel_id=1, source_target_pairs={{8,0},{16,8},{24,16},{9,1},{17,9},{25,17},{10,2},{18,10},{26,18},{... | collective-permute-start | bytes 1032200 | tf_op jit(solution)/shard_map/ppermute | solution.py:81
  16.7 5.4 %collective-permute-start.3 = (f32[2,3,1,1,2,512]{5,4,1,3,2,0:T(2,128)S(1)}, f32[2,3,1,1,2,512]{5,4,1,3,2,0:T(2,128)S(1)}, u32[]{:S(2)}, u32[]{:S(2)}) collective-permute-start(f32[2,3,1,1,2,512]{5,4,1,3,2,0:T(2,128)S(1)} %pad_maximum_fusion.8), channel_id=1, source_target_pairs={{0,2},{2,4},{4,6},{1,3},{3,5},{5,7},{8,10},{10,12},{12,14},{9,11},... | collective-permute-start | bytes 73736 | tf_op jit(solution)/shard_map/ppermute | solution.py:81
  18.1 5.5 %collective-permute-start.2 = (f32[7,3,1,1,2,512]{5,4,1,3,2,0:T(2,128)S(1)}, f32[7,3,1,1,2,512]{5,4,1,3,2,0:T(2,128)S(1)}, u32[]{:S(2)}, u32[]{:S(2)}) collective-permute-start(f32[7,3,1,1,2,512]{5,4,1,3,2,0:T(2,128)S(1)} %constant_dynamic-update-slice_fusion.7), channel_id=1, source_target_pairs={{2,0},{4,2},{6,4},{3,1},{5,3},{7,5},{10,8},{12,10},{14,12},{11,9},... | collective-permute-start | bytes 258056 | tf_op jit(solution)/shard_map/ppermute | solution.py:81
  23.7 6.0 %collective-permute-start.5 = (f32[2,3,1,4,1,512]{5,3,1,4,2,0:T(4,128)S(1)}, f32[2,3,1,4,1,512]{5,3,1,4,2,0:T(4,128)S(1)}, u32[]{:S(2)}, u32[]{:S(2)}) collective-permute-start(f32[2,3,1,4,1,512]{5,3,1,4,2,0:T(4,128)S(1)} %pad_maximum_fusion.7), channel_id=1, source_target_pairs={{0,1},{2,3},{4,5},{6,7},{8,9},{10,11},{12,13},{14,15},{16,17},{18,... | collective-permute-start | bytes 147464 | tf_op jit(solution)/shard_map/ppermute | solution.py:81
  25.2 5.4 %collective-permute-start.4 = (f32[7,3,1,4,1,512]{5,3,1,4,2,0:T(4,128)S(1)}, f32[7,3,1,4,1,512]{5,3,1,4,2,0:T(4,128)S(1)}, u32[]{:S(2)}, u32[]{:S(2)}) collective-permute-start(f32[7,3,1,4,1,512]{5,3,1,4,2,0:T(4,128)S(1)} %constant_dynamic-update-slice_fusion.14), channel_id=1, source_target_pairs={{1,0},{3,2},{5,4},{7,6},{9,8},{11,10},{13,12},{15,14},{17,16},{19,... | collective-permute-start | bytes 516104 | tf_op jit(solution)/shard_map/ppermute | solution.py:81
where the time goes:
time: 104 us; the launch traced here: 103 us
  Pallas kernels  67.3 us (65%)
  starting transfers between devices  16.3 us (16%)
  local copies, waits for them, and re-layouts  11.8 us (11%)
  other arithmetic  3.79 us (4%)
  waiting for transfers between devices  2.32 us (2%)
  between operations  1.93 us (2%)
    pallas_call x1, Pallas kernels, on_device(): pl.pallas_call(functools.partial(gather_kernel, devices), out_shape=jax.S...  39.8 us
    ppermute x6, starting transfers between devices, moved_targets(): came = lax.ppermute(slab, name, links)  16.3 us
    pallas_call x1, Pallas kernels, on_device(): pl.pallas_call(functools.partial(solve_kernel, bricks, devices), out_shap...  13.2 us
    pallas_call x1, Pallas kernels, on_device(): pl.pallas_call(functools.partial(turn_kernel, tiles), grid=(count // SLOT...  7.56 us
    pallas_call x1, Pallas kernels, on_device(): pl.pallas_call(functools.partial(assemble_kernel, tiles), out_shape=jax.S...  6.69 us
    reshape x4, local copies, waits for them, and re-layouts, flat(): return value.reshape(lead + (DIRS * tiles, points))  4.69 us
    dynamic_slice x4, local copies, waits for them, and re-layouts, mine(): lax.dynamic_slice(value, (0, me * tiles), (12, tiles))  2.88 us
    ppermute x6, waiting for transfers between devices, moved_targets(): came = lax.ppermute(slab, name, links)  2.32 us
  transfers between devices with their start and end apart: 6, of which 2 were waited for; matrix products, arithmetic and copies ran while one was open for 8% of the time, Pallas kernels for 0%

commit v1 on v0

v1 whole, which is shorter than its diff:
```python
import functools

import jax
import jax.numpy as jnp
from jax import lax
from jax.experimental import pallas as pl
from jax.experimental.pallas import tpu as pltpu
from jax.sharding import PartitionSpec as P

BLOCK = 256
ITERS = 10
SPACING = 0.5
DAMPING = 1.0
OFFSETS = (
    (1, 0, 0),
    (0, 1, 0),
    (0, 0, 1),
    (1, 1, -1),
    (1, -1, 1),
    (-1, 1, 1),
    (1, 1, 0),
    (1, 0, 1),
    (0, 1, 1),
    (1, 1, 1),
    (1, -1, 0),
    (0, 1, -1),
    (-1, 0, 1),
)
DIRS = len(OFFSETS)
LANES = 128
AXES = ("gx", "gy", "gz")
MESH = pl.DeviceIdType.MESH
VMEM_BYTES = 60 * 1024 * 1024

NORMAL_PAIRS = [(c, k) for c in range(3) for k in range(c, 3)]
POINT_PAIRS = [(e, k) for e in range(3) for k in range(e, 3)]
PAIR_ROWS = 96
THERE_ROWS = 36
SPILL = PAIR_ROWS + THERE_ROWS - LANES
SUMS = PAIR_ROWS + 2 * THERE_ROWS
SPILL_LANE = SPILL + THERE_ROWS
AFFINE_LANE = SPILL_LANE + SPILL * DIRS
SEND_ORDER = (3, 4, 5, 9, 7, 12, 0, 6, 10, 8, 11, 1, 2)
GROUPS = ((1, 2, 8, 11), (3, 4, 5, 9), (7, 12, 0, 6), (10,))


def normal_pair(c, k):
    return NORMAL_PAIRS.index((min(c, k), max(c, k)))


def point_pair(e, k):
    return POINT_PAIRS.index((min(e, k), max(e, k)))


def moves(step, length):
    if step == 0:
        return [(slice(0, length), slice(0, length), 0)]
    if step > 0:
        return [
            (slice(step, length), slice(0, length - step), 0),
            (slice(0, step), slice(length - step, length), -1),
        ]
    return [
        (slice(0, length + step), slice(-step, length), 0),
        (slice(length + step, length), slice(0, -step), 1),
    ]


def halo_pieces(bricks):
    pieces = []
    for d in SEND_ORDER:
        dx, dy, dz = OFFSETS[d]
        for y_from, y_to, y_step in moves(dy, bricks[1]):
            for z_from, z_to, z_step in moves(dz, bricks[2]):
                pieces.append((d, (y_from, z_from), (y_to, z_to), (-dx, y_step, z_step)))
    return pieces


def all_of(conditions):
    result = None
    for condition in conditions:
        result = condition if result is None else jnp.logical_and(result, condition)
    return result


def assemble_kernel(
    devices, bricks,
    count, affine, source, target, normal, weight,
    out,
    own_p, own_n, own_w, there, turned, acc,
    load_sem, stay_sem, halo_send, halo_recv,
    line_send, line_recv, side_send, side_recv, far_recv, core_send, core_recv,
):
    count_x, count_y, count_z = devices
    _, side_y, side_z = bricks
    at = tuple(lax.axis_index(name) for name in AXES)
    at_x, at_y, at_z = at
    pieces = halo_pieces(bricks)
    chunks = source.shape[3] // side_z

    def in_mesh(offset):
        return all_of(
            [
                (at[axis] + step >= 0) & (at[axis] + step < devices[axis])
                for axis, step in enumerate(offset)
                if step
            ]
        )

    def beside(offset):
        return tuple(
            jnp.clip(at[axis] + step, 0, devices[axis] - 1) if step else at[axis]
            for axis, step in enumerate(offset)
        )

    near_y = (at_y + 1 - 2 * (at_y % 2), (at_y + 2) % count_y)

    loads = []
    for g, group in enumerate(GROUPS):
        for d in group:
            loads.append(
                (
                    pltpu.make_async_copy(source.at[:, d], own_p.at[:, d], load_sem.at[0, d]),
                    pltpu.make_async_copy(normal.at[:, d], own_n.at[:, d], load_sem.at[1, d]),
                    pltpu.make_async_copy(weight.at[d], own_w.at[d], load_sem.at[2, d]),
                )
            )
            for copy in loads[-1]:
                copy.start()
    loads = dict(zip([d for group in GROUPS for d in group], loads))

    zeros = jnp.zeros(there.shape[2:], jnp.float32)
    for c in range(3):
        for d in range(DIRS):
            there[c, d] = zeros

    barrier = pltpu.get_barrier_semaphore()
    steps = {piece[3] for piece in pieces if any(piece[3])}
    steps |= {tuple(-s for s in step) for step in steps}
    steps |= {(1, 0, 0), (-1, 0, 0)}
    steps = sorted(steps)
    expected = 0
    for step in steps:
        there_is = in_mesh(step)

        @pl.when(there_is)
        def _(step=step):
            pl.semaphore_signal(barrier, inc=1, device_id=beside(step), device_id_type=MESH)

        expected = expected + there_is.astype(jnp.int32)
    for other in near_y:
        pl.semaphore_signal(barrier, inc=1, device_id=(at_x, other, at_z), device_id_type=MESH)
    for k in range(1, count_z):
        pl.semaphore_signal(
            barrier, inc=1, device_id=(at_x, at_y, (at_z + k) % count_z), device_id_type=MESH
        )
    pl.semaphore_wait(barrier, expected + (2 + count_z - 1))

    def spot(ref, d, where):
        return ref.at[:, d, where[0], :, where[1], :]

    def halo(i):
        d, start, end, step = pieces[i]
        return pltpu.make_async_remote_copy(
            src_ref=spot(target, d, start),
            dst_ref=spot(there, d, end),
            send_sem=halo_send.at[i],
            recv_sem=halo_recv.at[i],
            device_id=beside(step),
            device_id_type=MESH,
        )

    def stay(i):
        d, start, end, _ = pieces[i]
        return pltpu.make_async_copy(spot(target, d, start), spot(there, d, end), stay_sem.at[i])

    for i, piece in enumerate(pieces):
        if any(piece[3]):

            @pl.when(in_mesh(piece[3]))
            def _(i=i):
                halo(i).start()

        else:
            stay(i).start()

    inside = {}
    for axis in range(3):
        length = devices[axis] * bricks[axis]
        for place in range(bricks[axis]):
            for step in (-1, 1):
                ahead = at[axis] * bricks[axis] + place + step
                inside[axis, place, step] = ((ahead >= 0) & (ahead < length)).astype(jnp.int32)

    rows = chunks * side_z
    sub = lax.broadcasted_iota(jnp.int32, (rows, LANES), 0)
    lane = lax.broadcasted_iota(jnp.int32, (rows, LANES), 1)
    point = lane + LANES * (sub // side_z)

    def live_weight(d, y):
        limit = None
        for z in range(side_z):
            value = count[y, z, d] * BLOCK
            for axis, place in enumerate((0, y, z)):
                if OFFSETS[d][axis]:
                    value = value * inside[axis, place, OFFSETS[d][axis]]
            limit = value if limit is None else jnp.where(sub % side_z == z, value, limit)
        return jnp.where(point < limit, own_w[d, y], 0.0)

    def turn(parts):
        missing = LANES - rows * len(parts)
        if missing:
            parts = parts + [jnp.zeros((missing, LANES), jnp.float32)]
        return jnp.concatenate(parts, axis=0).T

    step = 32

    def summed(g, kinds):
        def body(chunk, carry):
            spots = pl.ds(pl.multiple_of(chunk * step, step), step)
            p = [turned[c, g, spots, :] for c in range(3)] + [None]
            q = [turned[7 + c, g, spots, :] for c in range(3)] + [None] if kinds == "there" else None
            n = [turned[3 + c, g, spots, :] for c in range(3)]
            w = turned[6, g, spots, :]

            def times(left, right):
                if left is None:
                    return right
                return left if right is None else left * right

            def add(row, value):
                acc[g, row] += jnp.sum(value.reshape(step // 8, 8, LANES), axis=0)

            wn = [w * n[c] for c in range(3)]
            weighted = [wn[c] * n[k] for c, k in NORMAL_PAIRS]
            if kinds == "here":
                for e in range(4):
                    for s in range(6):
                        add(s * 16 + e * 4 + 3, times(weighted[s], p[e]))
                for place, (e, k) in enumerate(POINT_PAIRS):
                    product = p[e] * p[k]
                    for s in range(6):
                        add(PAIR_ROWS + THERE_ROWS + s * 6 + place, weighted[s] * product)
            else:
                for e in range(4):
                    for k in range(3):
                        product = times(p[e], q[k])
                        for s in range(6):
                            add(s * 16 + e * 4 + k, weighted[s] * product)
                for place, (e, k) in enumerate(POINT_PAIRS):
                    product = q[e] * q[k]
                    for s in range(6):
                        add(PAIR_ROWS + s * 6 + place, weighted[s] * product)
            return carry

        lax.fori_loop(0, LANES // step, body, 0)

    acc[...] = jnp.zeros_like(acc)
    for g, group in enumerate(GROUPS):
        for d in group:
            for copy in loads[d]:
                copy.wait()
        for c in range(3):
            turned[c, g] = turn([own_p[c, d, y] for d in group for y in range(side_y)])
            turned[3 + c, g] = turn([own_n[c, d, y] for d in group for y in range(side_y)])
        turned[6, g] = turn([live_weight(d, y) for d in group for y in range(side_y)])
        summed(g, "here")

    there_rows = there.reshape(3, DIRS, side_y, rows, LANES)
    last = [None] * side_y
    for g, group in enumerate(GROUPS):
        for i, piece in enumerate(pieces):
            if piece[0] in group:
                if any(piece[3]):

                    @pl.when(in_mesh(tuple(-s for s in piece[3])))
                    def _(i=i):
                        halo(i).wait_recv()

                else:
                    stay(i).wait()
        for c in range(3):
            turned[7 + c, g] = turn([there_rows[c, d, y] for d in group for y in range(side_y)])
        summed(g, "there")
        whole = [jnp.sum(acc[g, r : r + 8], axis=1) for r in range(0, SUMS, 8)]
        main = jnp.concatenate(whole[: LANES // 8], axis=0).T
        rest = whole[LANES // 8 :] + [jnp.zeros((2 * LANES - SUMS, LANES), jnp.float32)]
        rest = jnp.concatenate(rest, axis=0).T

        def all_chunks(value):
            span = rows // 2
            while span >= side_z:
                value = value + pltpu.roll(value, span, 0)
                span //= 2
            return value

        for place, d in enumerate(group):
            for y in range(side_y):
                first = (place * side_y + y) * rows
                value = all_chunks(main[first : first + rows])
                out[d, at_x, at_y * side_y + y, at_z] = value[:side_z]
                value = all_chunks(rest[first : first + rows])
                spill = pltpu.roll(jnp.where(lane < SPILL, value, 0.0), SPILL_LANE + SPILL * d, 1)
                value = jnp.where(lane < SPILL, 0.0, value) + spill
                last[y] = value if last[y] is None else last[y] + value
    for y in range(side_y):
        pad = [jnp.zeros((side_z, AFFINE_LANE), jnp.float32), affine[y]]
        pad.append(jnp.zeros((side_z, LANES - AFFINE_LANE - affine.shape[2]), jnp.float32))
        out[DIRS, at_x, at_y * side_y + y, at_z] = last[y][:side_z] + jnp.concatenate(pad, axis=1)

    def part(x, y, z):
        return out.at[:, x, pl.ds(y * side_y, side_y), z]

    def send(x, y, z, send_sem, recv_sem, other):
        return pltpu.make_async_remote_copy(
            src_ref=part(x, y, z),
            dst_ref=part(x, y, z),
            send_sem=send_sem,
            recv_sem=recv_sem,
            device_id=other,
            device_id_type=MESH,
        )

    def along(x, sign):
        other = (jnp.clip(at_x + sign, 0, count_x - 1), at_y, at_z)
        return send(x, at_y, at_z, line_send.at[(sign + 1) // 2, x], line_recv.at[x], other)

    def across(x, way):
        other = (at_x, near_y[way], at_z)
        return send(x, at_y, at_z, side_send.at[way, x], side_recv.at[way, x], other)

    def across_in(x, way):
        other = (at_x, near_y[way], at_z)
        return send(x, near_y[way], at_z, side_send.at[way, x], side_recv.at[way, x], other)

    far_y = (near_y[0] + 2) % count_y

    def far_out(x, way):
        other = (at_x, near_y[1 - way], at_z)
        return send(x, near_y[way], at_z, side_send.at[2 + way, x], far_recv.at[x], other)

    def far_in(x):
        other = (at_x, near_y[0], at_z)
        return send(x, far_y, at_z, side_send.at[2, x], far_recv.at[x], other)

    def core_out(x, y, k):
        other = (at_x, at_y, (at_z + k) % count_z)
        return send(x, y, at_z, core_send.at[k - 1, x, y], core_recv.at[k - 1, x, y], other)

    def core_in(x, y, k):
        from_z = (at_z + count_z - k) % count_z
        other = (at_x, at_y, from_z)
        return send(x, y, from_z, core_send.at[k - 1, x, y], core_recv.at[k - 1, x, y], other)

    def to_cores(x, y):
        for k in range(1, count_z):
            core_out(x, y, k).start()

    def spread(x):
        across(x, 0).start()
        across(x, 1).start()
        to_cores(x, at_y)

    def arrived_side(x):
        for way in range(2):
            across_in(x, way).wait_recv()

            @pl.when(x % 2 == way)
            def _(way=way):
                far_out(x, way).start()

            to_cores(x, near_y[way])

    def arrived_far(x):
        far_in(x).wait_recv()
        to_cores(x, far_y)

    def both_ways(distance, body):
        if distance == 0:
            body(at_x, 0)
            return

        @pl.when(at_x - distance >= 0)
        def _():
            body(at_x - distance, 1)

        @pl.when(at_x + distance < count_x)
        def _():
            body(at_x + distance, -1)

    def own_out(sign):
        @pl.when((at_x + sign >= 0) & (at_x + sign < count_x))
        def _():
            along(at_x, sign).start()

    own_out(1)
    own_out(-1)
    spread(at_x)

    def line_arrived(x, sign):
        along(x, sign).wait_recv()

        @pl.when((at_x + sign >= 0) & (at_x + sign < count_x))
        def _():
            along(x, sign).start()

        spread(x)

    for distance in range(1, count_x + 2):
        if distance < count_x:
            both_ways(distance, line_arrived)
        if 0 <= distance - 1 < count_x:
            both_ways(distance - 1, lambda x, sign: arrived_side(x))
        if 0 <= distance - 2 < count_x:
            both_ways(distance - 2, lambda x, sign: arrived_far(x))

    def finish(x, carry):
        for sign in (1, -1):
            sent = (at_x + sign >= 0) & (at_x + sign < count_x)
            sent = sent & ((x <= at_x) if sign > 0 else (x >= at_x))

            @pl.when(sent)
            def _(sign=sign):
                along(x, sign).wait_send()

        for way in range(2):
            across(x, way).wait_send()

            @pl.when(x % 2 == way)
            def _(way=way):
                far_out(x, way).wait_send()

        def cores(y, inner):
            for k in range(1, count_z):
                core_in(x, y, k).wait_recv()
                core_out(x, y, k).wait_send()
            return inner

        lax.fori_loop(0, count_y, cores, 0)
        return carry

    lax.fori_loop(0, count_x, finish, 0)
    for i, piece in enumerate(pieces):
        if any(piece[3]):

            @pl.when(in_mesh(piece[3]))
            def _(i=i):
                halo(i).wait_send()


def solve_kernel(grid, bricks, anchor, parts, update_out, residual_out, blocks, turned, tiles):
    count_x, count_y, count_z = grid
    _, side_y, side_z = bricks
    half = blocks.shape[3]
    plane = count_y * count_z
    lane = lax.broadcasted_iota(jnp.int32, (8, half), 1)
    sub = lax.broadcasted_iota(jnp.int32, (8, half), 0)
    column = sub % 4
    low = sub < 4

    for r in range(DIRS + 1):
        for start in range(0, half, LANES):
            spots = pl.ds(start, LANES)
            first = parts[r, pl.ds(start, LANES), :].T
            second = parts[r, pl.ds(half + start, LANES), :].T
            for i in range(LANES // 4):
                blocks[r, i, :, spots] = jnp.concatenate(
                    [first[4 * i : 4 * i + 4], second[4 * i : 4 * i + 4]], axis=0
                )

    def ahead(value, offset, sign=1):
        shift = sign * (offset[0] * plane + offset[1] * count_z + offset[2])
        result = pltpu.roll(value, (-shift) % half, 1)
        if offset[0]:
            stays = (lane + shift >= 0) & (lane + shift < half)
            result = jnp.where(stays, result, pltpu.roll(result, 4, 0))
        return result

    def spread(value, e):
        return jnp.where(low, value[e : e + 1], value[4 + e : 5 + e])

    def butterfly(first, second, span):
        takes_first = (column & span) == 0
        return jnp.where(takes_first, first, pltpu.roll(second, span, 0)) + jnp.where(
            takes_first, pltpu.roll(first, 8 - span, 0), second
        )

    def columns_summed(four):
        return butterfly(butterfly(four[0], four[1], 1), butterfly(four[2], four[3], 1), 2)

    def total(terms):
        terms = list(terms)
        while len(terms) > 1:
            terms = [
                terms[i] + terms[i + 1] if i + 1 < len(terms) else terms[i]
                for i in range(0, len(terms), 2)
            ]
        return terms[0]

    def transposed(d, spreads):
        return [
            total(
                blocks[d, normal_pair(c, k) * 4 + e] * spreads[c][e]
                for c in range(3)
                for e in range(4)
            )
            for k in range(3)
        ]

    def operate(vector, shifted=False):
        spreads = [[spread(vector[c], e) for e in range(4)] for c in range(3)]
        result = transposed(DIRS, spreads)
        sums = [[None] * 4 for _ in range(3)]
        back = [None] * 3
        for d, offset in enumerate(OFFSETS):
            near = [ahead(vector[k], offset) for k in range(3)]
            here = spreads
            if shifted:
                near = [
                    near[k] + jnp.where(column == 3, SPACING * offset[k], 0.0) for k in range(3)
                ]
                here = [
                    spreads[c][:3] + [spreads[c][3] - SPACING * offset[c]] for c in range(3)
                ]
            sent = transposed(d, here)
            for c in range(3):
                for e in range(4):
                    term = total(
                        blocks[d, normal_pair(c, k) * 4 + e] * near[k] for k in range(3)
                    )
                    sums[c][e] = term if sums[c][e] is None else sums[c][e] + term
            for k in range(3):
                term = ahead(sent[k], offset, -1)
                back[k] = term if back[k] is None else back[k] + term
        return [result[k] - back[k] - columns_summed(sums[k]) for k in range(3)]

    def rows_of(value):
        return [jnp.concatenate([value[f : f + 1], value[4 + f : 5 + f]], axis=0) for f in range(4)]

    both = []
    for g in range(THERE_ROWS // 4):
        value = blocks[DIRS, SPILL // 4 + g]
        for d, offset in enumerate(OFFSETS):
            group = PAIR_ROWS // 4 + g
            if group < LANES // 4:
                term = blocks[d, group]
            else:
                term = blocks[DIRS, SPILL_LANE // 4 + d]
            value = value + ahead(term, offset, -1)
        both.append(value)
    unit = [(column == k).astype(jnp.float32) for k in range(3)]
    affine = [blocks[DIRS, AFFINE_LANE // 4 + k] + unit[k] for k in range(3)]
    diagonal = []
    for s in range(6):
        edge = None
        for d, offset in enumerate(OFFSETS):
            term = ahead(blocks[d, s * 4 + 3], offset, -1)
            edge = term if edge is None else edge + term
        for e in range(4):
            term = total(blocks[d, s * 4 + e] for d in range(DIRS))
            edge = edge + jnp.where(column == e, spread(term, 3), 0.0)
        for e in range(3):
            value = spread(edge, e)
            for f in range(3):
                i = s * 6 + point_pair(e, f)
                value = jnp.where(column == f, spread(both[i // 4], i % 4), value)
            diagonal.append(value)
        diagonal.append(edge)
    for i, value in enumerate(diagonal):
        blocks[DIRS, i] = value

    flat = lane + jnp.where(low, 0, half)
    keep = (flat != anchor[0]).astype(jnp.float32)
    rhs = [-(keep * value) for value in operate(affine, True)]

    matrix = []
    for c in range(3):
        for e in range(4):
            row = []
            for k in range(3):
                value = blocks[DIRS, normal_pair(c, k) * 4 + e]
                if c == k:
                    eye = (column == e).astype(jnp.float32)
                    damped = value + DAMPING * eye
                    blocks_value = keep * damped + (1.0 - keep) * eye
                else:
                    blocks_value = keep * value
                row.append(blocks_value)
            matrix.append(row)
    for s, (c, k) in enumerate(NORMAL_PAIRS):
        if c == k:
            for e in range(4):
                value = blocks[DIRS, s * 4 + e]
                blocks[DIRS, s * 4 + e] = value + DAMPING * (column == e).astype(jnp.float32)
    for pivot in range(12):
        c, e = divmod(pivot, 4)
        here = matrix[pivot]
        factor = 1.0 / spread(here[c], e)
        at_pivot = column == e
        scaled = [here[k] * factor for k in range(3)]
        scaled[c] = jnp.where(at_pivot, factor, scaled[c])
        for a in range(12):
            if a == pivot:
                matrix[a] = scaled
            else:
                row = list(matrix[a])
                entry = spread(row[c], e)
                row[c] = jnp.where(at_pivot, 0.0, row[c])
                matrix[a] = [row[k] - entry * scaled[k] for k in range(3)]
    for a in range(12):
        for k in range(3):
            turned[a * 3 + k] = matrix[a][k]

    def precondition(vector):
        spreads = [[spread(vector[c], e) for e in range(4)] for c in range(3)]
        return [
            total(
                turned[(4 * c + e) * 3 + k] * spreads[c][e] for c in range(3) for e in range(4)
            )
            for k in range(3)
        ]

    def dot(left, right):
        return jnp.sum(total(left[k] * right[k] for k in range(3)), keepdims=True)

    first = precondition(rhs)

    def step(_, carry):
        update, residual, direction, inner_now = carry
        along = [keep * value for value in operate(direction)]
        alpha = inner_now / dot(direction, along)
        update = [update[k] + alpha * direction[k] for k in range(3)]
        residual = [residual[k] - alpha * along[k] for k in range(3)]
        scaled = precondition(residual)
        inner_next = dot(residual, scaled)
        beta = inner_next / inner_now
        direction = [scaled[k] + beta * direction[k] for k in range(3)]
        return update, residual, direction, inner_next

    start = ([jnp.zeros_like(value) for value in rhs], rhs, first, dot(rhs, first))
    update, residual, _, _ = lax.fori_loop(0, ITERS, step, start)

    at_x, at_y, at_z = (lax.axis_index(name) for name in AXES)
    upper = at_x // (count_x // 2)
    base = (at_x - upper * (count_x // 2)) * plane + at_y * side_y * count_z + at_z * side_z
    chosen = [jnp.where(upper == 0, v[:4], v[4:]) for v in update + residual]
    chosen.append(jnp.zeros((LANES - 24, half), jnp.float32))
    tall = jnp.concatenate(chosen, axis=0)
    for start in range(0, half, LANES):
        tiles[pl.ds(start, LANES), :] = tall[:, start : start + LANES].T
    for y in range(side_y):
        rows = tiles[pl.ds(base + y * count_z, side_z), :]
        update_out[y] = rows[:, :12]
        residual_out[y] = rows[:, 12:24]


def on_device(source_points, target_points, normals, weights, blocks, affines, anchor):
    bricks = source_points.shape[2:5]
    points = source_points.shape[5]
    devices = tuple(lax.axis_size(name) for name in AXES)
    grid = tuple(devices[axis] * bricks[axis] for axis in range(3))
    span = grid[0] * grid[1] * grid[2]
    chunks = points // LANES
    rows = chunks * bricks[2]
    assert bricks[0] == 1 and rows == 8 and grid[0] % 2 == 0 and devices[1] == 4
    assert span % (2 * LANES) == 0 and len(GROUPS[0]) * bricks[1] * rows == LANES

    def split(value):
        lead = value.shape[:-5]
        value = value.reshape(lead + (DIRS, bricks[1], bricks[2], chunks, LANES))
        return jnp.swapaxes(value, -3, -2)

    def filled(value):
        value = split(value)
        return value.reshape(value.shape[:-3] + (rows, LANES))

    params = functools.partial(pltpu.CompilerParams, vmem_limit_bytes=VMEM_BYTES)
    vmem = pl.BlockSpec(memory_space=pltpu.VMEM)
    smem = pl.BlockSpec(memory_space=pltpu.SMEM)
    anywhere = pl.BlockSpec(memory_space=pl.ANY)
    pieces = len(halo_pieces(bricks))
    dma = pltpu.SemaphoreType.DMA
    own = (DIRS, bricks[1], rows, LANES)
    gathered = pl.pallas_call(
        functools.partial(assemble_kernel, devices, bricks),
        out_shape=jax.ShapeDtypeStruct(
            (DIRS + 1, grid[0], grid[1], devices[2], bricks[2], LANES), jnp.float32
        ),
        in_specs=[smem, vmem] + [anywhere] * 4,
        out_specs=vmem,
        scratch_shapes=[
            pltpu.VMEM((3,) + own, jnp.float32),
            pltpu.VMEM((3,) + own, jnp.float32),
            pltpu.VMEM(own, jnp.float32),
            pltpu.VMEM((3, DIRS, bricks[1], chunks, bricks[2], LANES), jnp.float32),
            pltpu.VMEM((10, len(GROUPS), LANES, LANES), jnp.float32),
            pltpu.VMEM((len(GROUPS), SUMS, 8, LANES), jnp.float32),
            dma((3, DIRS)),
            dma((pieces,)),
            dma((pieces,)),
            dma((pieces,)),
            dma((2, devices[0])),
            dma((devices[0],)),
            dma((4, devices[0])),
            dma((2, devices[0])),
            dma((devices[0],)),
            dma((devices[2] - 1, devices[0], devices[1])),
            dma((devices[2] - 1, devices[0], devices[1])),
        ],
        compiler_params=params(collective_id=0, has_side_effects=True),
        name="assemble",
    )(
        jnp.transpose(blocks, (1, 2, 3, 0)).reshape(bricks[1], bricks[2], DIRS),
        jnp.transpose(affines, (1, 2, 3, 0)).reshape(bricks[1], bricks[2], 12),
        filled(source_points),
        split(target_points),
        filled(normals),
        filled(weights),
    )
    update, residual = pl.pallas_call(
        functools.partial(solve_kernel, grid, bricks),
        out_shape=[jax.ShapeDtypeStruct(bricks[1:] + (12,), jnp.float32)] * 2,
        in_specs=[smem, vmem],
        out_specs=[vmem, vmem],
        scratch_shapes=[
            pltpu.VMEM((DIRS + 1, LANES // 4, 8, span // 2), jnp.float32),
            pltpu.VMEM((36, 8, span // 2), jnp.float32),
            pltpu.VMEM((span // 2, LANES), jnp.float32),
        ],
        compiler_params=params(),
        name="solve",
    )(anchor, gathered.reshape(DIRS + 1, span, LANES))

    def placed(value):
        return jnp.transpose(value, (2, 0, 1)).reshape((12,) + bricks)

    return placed(update), placed(residual)


def solution(mesh):
    points = P(None, None, "gx", "gy", "gz", None)
    tiles = P(None, "gx", "gy", "gz")
    return jax.shard_map(
        on_device,
        mesh=mesh,
        in_specs=(points, points, points, P(None, "gx", "gy", "gz", None), tiles, tiles, P()),
        out_specs=(tiles, tiles),
        check_vma=False,
    )
```

time: 104 us -> 47 us (0.45)
  the two profiles are of different devices: /device:TPU:15 before, /device:TPU:0 now
where the time goes in v1:
time: 47 us; the launch traced here: 46.8 us
  Pallas kernels  45.5 us (97%)
  between operations  1.29 us (3%)
    pallas_call x1, Pallas kernels, on_device(): pl.pallas_call(functools.partial(assemble_kernel, devices, bricks), out_s...  36.3 us
    pallas_call x1, Pallas kernels, on_device(): pl.pallas_call(functools.partial(solve_kernel, grid, bricks), out_shape=[...  9.15 us

profile of v1, /device:TPU:0, one launch (start us, length us, event | category | flops | bytes accessed | tf_op | source)
XLA Modules:
  0.0 46.8 jit_solution(8385189339873961565)
XLA Ops:
  1.3 36.3 %assemble.1 = f32[14,4,16,2,2,128]{5,4,3,2,1,0:T(2,128)} custom-call(s32[4,2,13]{2,1,0:T(2,128)} %bitcast.36, f32[4,2,12]{2,1,0:T(2,128)} %bitcast.37, f32[3,13,4,8,128]{4,3,2,1,0:T(8,128)} %bitcast.32, f32[3,13,4,4,2,128]{5,4,3,2,1,0:T(2,128)} %bitcast.33, f32[3,13,4,8,128]{4,3,2,1,0:T(8,128)} %bitcast.34, f32[13,4,8,128]{3,2,1,0:T(8,128)} %bitcast.35), custom_call_target="tpu_custom_call" | custom-call | tf_op jit(solution)/shard_map/assemble/pallas_call | solution.py:684
  37.6 9.1 %solve.1 = (f32[4,2,12]{2,1,0:T(2,128)}, f32[4,2,12]{2,1,0:T(2,128)}) custom-call(s32[1]{0:T(128)S(6)} %copy.18.anchor, f32[14,256,128]{2,1,0:T(8,128)} %bitcast.31), custom_call_target="tpu_custom_call" | custom-call | tf_op jit(solution)/shard_map/solve/pallas_call | solution.py:720

commit v2 on v1

v2 whole, which is shorter than its diff:
```python
import functools

import jax
import jax.numpy as jnp
from jax import lax
from jax.experimental import pallas as pl
from jax.experimental.pallas import tpu as pltpu
from jax.sharding import PartitionSpec as P

BLOCK = 256
ITERS = 10
SPACING = 0.5
DAMPING = 1.0
OFFSETS = (
    (1, 0, 0),
    (0, 1, 0),
    (0, 0, 1),
    (1, 1, -1),
    (1, -1, 1),
    (-1, 1, 1),
    (1, 1, 0),
    (1, 0, 1),
    (0, 1, 1),
    (1, 1, 1),
    (1, -1, 0),
    (0, 1, -1),
    (-1, 0, 1),
)
DIRS = len(OFFSETS)
LANES = 128
AXES = ("gx", "gy", "gz")
MESH = pl.DeviceIdType.MESH
VMEM_BYTES = 60 * 1024 * 1024

NORMAL_PAIRS = [(c, k) for c in range(3) for k in range(c, 3)]
POINT_PAIRS = [(e, k) for e in range(3) for k in range(e, 3)]
PAIR_ROWS = 96
THERE_ROWS = 36
SPILL = PAIR_ROWS + THERE_ROWS - LANES
SUMS = PAIR_ROWS + 2 * THERE_ROWS
SPILL_LANE = SPILL + THERE_ROWS
AFFINE_LANE = SPILL_LANE + SPILL * DIRS
SEND_ORDER = (3, 4, 5, 9, 7, 12, 0, 6, 10, 8, 11, 1, 2)
GROUPS = ((1, 2, 8, 11), (3, 4, 5, 9), (7, 12, 0, 6), (10,))
ROW_OF = {d: place for place, d in enumerate(d for group in GROUPS for d in group)}
DIRECTION_OF = {place: d for d, place in ROW_OF.items()}
CHUNKS = ((0, 4), (4, 8), (8, 12), (12, DIRS + 1))
LINE_DIRECT = (True, True, True, True)
FAR_DIRECT = (True, True, True, True)
ROUNDS_BEFORE = ((), (0,), (0, 0), (0, 0, 0))


def normal_pair(c, k):
    return NORMAL_PAIRS.index((min(c, k), max(c, k)))


def point_pair(e, k):
    return POINT_PAIRS.index((min(e, k), max(e, k)))


def moves(step, length):
    if step == 0:
        return [(slice(0, length), slice(0, length), 0)]
    if step > 0:
        return [
            (slice(step, length), slice(0, length - step), 0),
            (slice(0, step), slice(length - step, length), -1),
        ]
    return [
        (slice(0, length + step), slice(-step, length), 0),
        (slice(length + step, length), slice(0, -step), 1),
    ]


def halo_pieces(bricks):
    pieces = []
    for d in SEND_ORDER:
        dx, dy, dz = OFFSETS[d]
        for y_from, y_to, y_step in moves(dy, bricks[1]):
            for z_from, z_to, z_step in moves(dz, bricks[2]):
                pieces.append((d, (y_from, z_from), (y_to, z_to), (-dx, y_step, z_step)))
    return pieces


def all_of(conditions):
    result = None
    for condition in conditions:
        result = condition if result is None else jnp.logical_and(result, condition)
    return result


class Solver:
    def __init__(self, devices, bricks, blocks, turned):
        self.grid = tuple(devices[axis] * bricks[axis] for axis in range(3))
        self.bricks = bricks
        self.blocks = blocks
        self.turned = turned

    def load(self, parts, r):
        half = self.blocks.shape[3]
        many = LANES // 8
        d = DIRECTION_OF.get(r, DIRS)
        for start in range(0, half, LANES):
            first = parts[pl.ds(start // 8, many), r].reshape(LANES, LANES).T
            second = parts[pl.ds((half + start) // 8, many), r].reshape(LANES, LANES).T
            for i in range(LANES // 4):
                self.blocks[d, i, :, pl.ds(start, LANES)] = jnp.concatenate(
                    [first[4 * i : 4 * i + 4], second[4 * i : 4 * i + 4]], axis=0
                )

    def run(self, anchor, update_out, residual_out, tiles):
        solve(self.grid, self.bricks, anchor, update_out, residual_out, self.blocks, self.turned, tiles)


def solve(grid, bricks, anchor, update_out, residual_out, blocks, turned, tiles):
    count_x, count_y, count_z = grid
    _, side_y, side_z = bricks
    half = blocks.shape[3]
    line = count_y * side_z
    plane = count_x * line
    lane = lax.broadcasted_iota(jnp.int32, (8, half), 1)
    sub = lax.broadcasted_iota(jnp.int32, (8, half), 0)
    column = sub % 4
    low = sub < 4

    def ahead(value, offset, sign=1):
        dx, dy, dz = (sign * part for part in offset)
        shift = dx * line + dy * side_z + dz
        result = pltpu.roll(value, (-shift) % half, 1)
        if dz:
            cross = shift + dz * (plane - side_z)
            other = pltpu.roll(value, (-cross) % half, 1)
            swapped = pltpu.roll(other, 4, 0)
            if plane != half:
                stays = (lane + cross >= 0) & (lane + cross < half)
                swapped = jnp.where(stays, other, swapped)
            edge = side_z - 1 if dz > 0 else 0
            result = jnp.where(lane % side_z == edge, swapped, result)
        return result

    def spread(value, e):
        return jnp.where(low, value[e : e + 1], value[4 + e : 5 + e])

    def butterfly(first, second, span):
        takes_first = (column & span) == 0
        return jnp.where(takes_first, first, pltpu.roll(second, span, 0)) + jnp.where(
            takes_first, pltpu.roll(first, 8 - span, 0), second
        )

    def columns_summed(four):
        return butterfly(butterfly(four[0], four[1], 1), butterfly(four[2], four[3], 1), 2)

    def total(terms):
        terms = list(terms)
        while len(terms) > 1:
            terms = [
                terms[i] + terms[i + 1] if i + 1 < len(terms) else terms[i]
                for i in range(0, len(terms), 2)
            ]
        return terms[0]

    def transposed(d, spreads):
        return [
            total(
                blocks[d, normal_pair(c, k) * 4 + e] * spreads[c][e]
                for c in range(3)
                for e in range(4)
            )
            for k in range(3)
        ]

    def operate(vector, shifted=False):
        spreads = [[spread(vector[c], e) for e in range(4)] for c in range(3)]
        result = transposed(DIRS, spreads)
        sums = [[None] * 4 for _ in range(3)]
        back = [None] * 3
        for d, offset in enumerate(OFFSETS):
            near = [ahead(vector[k], offset) for k in range(3)]
            here = spreads
            if shifted:
                near = [
                    near[k] + jnp.where(column == 3, SPACING * offset[k], 0.0) for k in range(3)
                ]
                here = [
                    spreads[c][:3] + [spreads[c][3] - SPACING * offset[c]] for c in range(3)
                ]
            sent = transposed(d, here)
            for c in range(3):
                for e in range(4):
                    term = total(
                        blocks[d, normal_pair(c, k) * 4 + e] * near[k] for k in range(3)
                    )
                    sums[c][e] = term if sums[c][e] is None else sums[c][e] + term
            for k in range(3):
                term = ahead(sent[k], offset, -1)
                back[k] = term if back[k] is None else back[k] + term
        return [result[k] - back[k] - columns_summed(sums[k]) for k in range(3)]

    def rows_of(value):
        return [jnp.concatenate([value[f : f + 1], value[4 + f : 5 + f]], axis=0) for f in range(4)]

    both = []
    for g in range(THERE_ROWS // 4):
        value = blocks[DIRS, SPILL // 4 + g]
        for d, offset in enumerate(OFFSETS):
            group = PAIR_ROWS // 4 + g
            if group < LANES // 4:
                term = blocks[d, group]
            else:
                term = blocks[DIRS, SPILL_LANE // 4 + d]
            value = value + ahead(term, offset, -1)
        both.append(value)
    unit = [(column == k).astype(jnp.float32) for k in range(3)]
    affine = [blocks[DIRS, AFFINE_LANE // 4 + k] + unit[k] for k in range(3)]
    diagonal = []
    for s in range(6):
        edge = None
        for d, offset in enumerate(OFFSETS):
            term = ahead(blocks[d, s * 4 + 3], offset, -1)
            edge = term if edge is None else edge + term
        for e in range(4):
            term = total(blocks[d, s * 4 + e] for d in range(DIRS))
            edge = edge + jnp.where(column == e, spread(term, 3), 0.0)
        for e in range(3):
            value = spread(edge, e)
            for f in range(3):
                i = s * 6 + point_pair(e, f)
                value = jnp.where(column == f, spread(both[i // 4], i % 4), value)
            diagonal.append(value)
        diagonal.append(edge)
    for i, value in enumerate(diagonal):
        blocks[DIRS, i] = value

    brick_z = lane // plane + jnp.where(low, 0, half // plane)
    flat = lane % plane // side_z * count_z + brick_z * side_z + lane % side_z
    keep = (flat != anchor[0]).astype(jnp.float32)
    rhs = [-(keep * value) for value in operate(affine, True)]

    matrix = []
    for c in range(3):
        for e in range(4):
            row = []
            for k in range(3):
                value = blocks[DIRS, normal_pair(c, k) * 4 + e]
                if c == k:
                    eye = (column == e).astype(jnp.float32)
                    damped = value + DAMPING * eye
                    blocks_value = keep * damped + (1.0 - keep) * eye
                else:
                    blocks_value = keep * value
                row.append(blocks_value)
            matrix.append(row)
    for s, (c, k) in enumerate(NORMAL_PAIRS):
        if c == k:
            for e in range(4):
                value = blocks[DIRS, s * 4 + e]
                blocks[DIRS, s * 4 + e] = value + DAMPING * (column == e).astype(jnp.float32)
    for pivot in range(12):
        c, e = divmod(pivot, 4)
        here = matrix[pivot]
        factor = 1.0 / spread(here[c], e)
        at_pivot = column == e
        scaled = [here[k] * factor for k in range(3)]
        scaled[c] = jnp.where(at_pivot, factor, scaled[c])
        for a in range(12):
            if a == pivot:
                matrix[a] = scaled
            else:
                row = list(matrix[a])
                entry = spread(row[c], e)
                row[c] = jnp.where(at_pivot, 0.0, row[c])
                matrix[a] = [row[k] - entry * scaled[k] for k in range(3)]
    for a in range(12):
        for k in range(3):
            turned[a * 3 + k] = matrix[a][k]

    def precondition(vector):
        spreads = [[spread(vector[c], e) for e in range(4)] for c in range(3)]
        return [
            total(
                turned[(4 * c + e) * 3 + k] * spreads[c][e] for c in range(3) for e in range(4)
            )
            for k in range(3)
        ]

    def dot(left, right):
        return jnp.sum(total(left[k] * right[k] for k in range(3)), keepdims=True)

    first = precondition(rhs)

    def step(_, carry):
        update, residual, direction, inner_now = carry
        along = [keep * value for value in operate(direction)]
        alpha = inner_now / dot(direction, along)
        update = [update[k] + alpha * direction[k] for k in range(3)]
        residual = [residual[k] - alpha * along[k] for k in range(3)]
        scaled = precondition(residual)
        inner_next = dot(residual, scaled)
        beta = inner_next / inner_now
        direction = [scaled[k] + beta * direction[k] for k in range(3)]
        return update, residual, direction, inner_next

    start = ([jnp.zeros_like(value) for value in rhs], rhs, first, dot(rhs, first))
    update, residual, _, _ = lax.fori_loop(0, ITERS, step, start)

    at_x, at_y, at_z = (lax.axis_index(name) for name in AXES)
    bricks_half = half // plane
    upper = at_z // bricks_half
    base = (at_z - upper * bricks_half) * plane + at_x * line + at_y * side_y * side_z
    chosen = [jnp.where(upper == 0, v[:4], v[4:]) for v in update + residual]
    chosen.append(jnp.zeros((LANES - 24, half), jnp.float32))
    tall = jnp.concatenate(chosen, axis=0)
    for start in range(0, half, LANES):
        tiles[pl.ds(start, LANES), :] = tall[:, start : start + LANES].T
    rows = tiles[pl.ds(pl.multiple_of(base, 8), side_y * side_z), :]
    for y in range(side_y):
        row = rows[y * side_z : (y + 1) * side_z]
        update_out[y] = row[:, :12]
        residual_out[y] = row[:, 12:24]


def step_kernel(
    devices, bricks,
    anchor, count_in, affine_in, source, target, normal, weight,
    update_out, residual_out,
    count, affine, out, blocks, turned_inverse, tiles, small_sem,
    own_p, own_n, own_w, there, turned, acc,
    load_sem, stay_sem, halo_send, halo_recv,
    line_send, direct_send, line_recv, side_send, side_recv, core_send, core_recv,
):
    count_x, count_y, count_z = devices
    _, side_y, side_z = bricks
    at = tuple(lax.axis_index(name) for name in AXES)
    at_x, at_y, at_z = at
    pieces = halo_pieces(bricks)
    chunks = source.shape[3] // side_z

    def in_mesh(offset):
        return all_of(
            [
                (at[axis] + step >= 0) & (at[axis] + step < devices[axis])
                for axis, step in enumerate(offset)
                if step
            ]
        )

    def beside(offset):
        return tuple(
            jnp.clip(at[axis] + step, 0, devices[axis] - 1) if step else at[axis]
            for axis, step in enumerate(offset)
        )

    near_y = [at_y + 1 - 2 * (at_y % 2), (at_y + 2) % count_y]
    near_y.append((near_y[0] + 2) % count_y)

    small = (
        pltpu.make_async_copy(count_in, count, small_sem.at[0]),
        pltpu.make_async_copy(affine_in, affine, small_sem.at[1]),
    )
    for copy in small:
        copy.start()

    loads = []
    for g, group in enumerate(GROUPS):
        for d in group:
            loads.append(
                (
                    pltpu.make_async_copy(source.at[:, d], own_p.at[:, d], load_sem.at[0, d]),
                    pltpu.make_async_copy(normal.at[:, d], own_n.at[:, d], load_sem.at[1, d]),
                    pltpu.make_async_copy(weight.at[d], own_w.at[d], load_sem.at[2, d]),
                )
            )
            for copy in loads[-1]:
                copy.start()
    loads = dict(zip([d for group in GROUPS for d in group], loads))

    zeros = jnp.zeros(there.shape[2:], jnp.float32)
    for c in range(3):
        for d in range(DIRS):
            there[c, d] = zeros

    barrier = pltpu.get_barrier_semaphore()
    steps = {piece[3] for piece in pieces if any(piece[3])}
    steps |= {tuple(-s for s in step) for step in steps}
    steps |= {(k, 0, 0) for k in range(1 - count_x, count_x) if k}
    steps = sorted(steps)
    expected = 0
    for step in steps:
        there_is = in_mesh(step)

        @pl.when(there_is)
        def _(step=step):
            pl.semaphore_signal(barrier, inc=1, device_id=beside(step), device_id_type=MESH)

        expected = expected + there_is.astype(jnp.int32)
    for other in near_y:
        pl.semaphore_signal(barrier, inc=1, device_id=(at_x, other, at_z), device_id_type=MESH)
    for k in range(1, count_z):
        pl.semaphore_signal(
            barrier, inc=1, device_id=(at_x, at_y, (at_z + k) % count_z), device_id_type=MESH
        )
    pl.semaphore_wait(barrier, expected + (3 + count_z - 1))

    def spot(ref, d, where):
        return ref.at[:, d, where[0], :, where[1], :]

    def halo(i):
        d, start, end, step = pieces[i]
        return pltpu.make_async_remote_copy(
            src_ref=spot(target, d, start),
            dst_ref=spot(there, d, end),
            send_sem=halo_send.at[i],
            recv_sem=halo_recv.at[i],
            device_id=beside(step),
            device_id_type=MESH,
        )

    def stay(i):
        d, start, end, _ = pieces[i]
        return pltpu.make_async_copy(spot(target, d, start), spot(there, d, end), stay_sem.at[i])

    for i, piece in enumerate(pieces):
        if any(piece[3]):

            @pl.when(in_mesh(piece[3]))
            def _(i=i):
                halo(i).start()

        else:
            stay(i).start()

    inside = {}
    for axis in range(3):
        length = devices[axis] * bricks[axis]
        for place in range(bricks[axis]):
            for step in (-1, 1):
                ahead = at[axis] * bricks[axis] + place + step
                inside[axis, place, step] = ((ahead >= 0) & (ahead < length)).astype(jnp.int32)

    for copy in small:
        copy.wait()
    rows = chunks * side_z
    sub = lax.broadcasted_iota(jnp.int32, (rows, LANES), 0)
    lane = lax.broadcasted_iota(jnp.int32, (rows, LANES), 1)
    point = lane + LANES * (sub // side_z)

    def live_weight(d, y):
        limit = None
        for z in range(side_z):
            value = count[y, z, d] * BLOCK
            for axis, place in enumerate((0, y, z)):
                if OFFSETS[d][axis]:
                    value = value * inside[axis, place, OFFSETS[d][axis]]
            limit = value if limit is None else jnp.where(sub % side_z == z, value, limit)
        return jnp.where(point < limit, own_w[d, y], 0.0)

    def turn(parts):
        missing = LANES - rows * len(parts)
        if missing:
            parts = parts + [jnp.zeros((missing, LANES), jnp.float32)]
        return jnp.concatenate(parts, axis=0).T

    step = 32

    def summed(g, kinds):
        def body(chunk, carry):
            spots = pl.ds(pl.multiple_of(chunk * step, step), step)
            p = [turned[c, g, spots, :] for c in range(3)] + [None]
            q = [turned[7 + c, g, spots, :] for c in range(3)] + [None] if kinds == "there" else None
            n = [turned[3 + c, g, spots, :] for c in range(3)]
            w = turned[6, g, spots, :]

            def times(left, right):
                if left is None:
                    return right
                return left if right is None else left * right

            def add(row, value):
                acc[g, row] += jnp.sum(value.reshape(step // 8, 8, LANES), axis=0)

            wn = [w * n[c] for c in range(3)]
            weighted = [wn[c] * n[k] for c, k in NORMAL_PAIRS]
            if kinds == "here":
                for e in range(4):
                    for s in range(6):
                        add(s * 16 + e * 4 + 3, times(weighted[s], p[e]))
                for place, (e, k) in enumerate(POINT_PAIRS):
                    product = p[e] * p[k]
                    for s in range(6):
                        add(PAIR_ROWS + THERE_ROWS + s * 6 + place, weighted[s] * product)
            else:
                for e in range(4):
                    for k in range(3):
                        product = times(p[e], q[k])
                        for s in range(6):
                            add(s * 16 + e * 4 + k, weighted[s] * product)
                for place, (e, k) in enumerate(POINT_PAIRS):
                    product = q[e] * q[k]
                    for s in range(6):
                        add(PAIR_ROWS + s * 6 + place, weighted[s] * product)
            return carry

        lax.fori_loop(0, LANES // step, body, 0)

    acc[...] = jnp.zeros_like(acc)

    def here(g):
        group = GROUPS[g]
        for d in group:
            for copy in loads[d]:
                copy.wait()
        for c in range(3):
            turned[c, g] = turn([own_p[c, d, y] for d in group for y in range(side_y)])
            turned[3 + c, g] = turn([own_n[c, d, y] for d in group for y in range(side_y)])
        turned[6, g] = turn([live_weight(d, y) for d in group for y in range(side_y)])
        summed(g, "here")

    there_rows = there.reshape(3, DIRS, side_y, rows, LANES)
    last = [None] * side_y
    mine = out.at[at_z, at_x, at_y]

    def tiles_of(values):
        result = values[0]
        for y in range(1, side_y):
            result = jnp.where(sub // side_z == y, values[y], result)
        return result

    def there_sums(g):
        group = GROUPS[g]
        for i, piece in enumerate(pieces):
            if piece[0] in group:
                if any(piece[3]):

                    @pl.when(in_mesh(tuple(-s for s in piece[3])))
                    def _(i=i):
                        halo(i).wait_recv()

                else:
                    stay(i).wait()
        for c in range(3):
            turned[7 + c, g] = turn([there_rows[c, d, y] for d in group for y in range(side_y)])
        summed(g, "there")
        whole = [jnp.sum(acc[g, r : r + 8], axis=1) for r in range(0, SUMS, 8)]
        main = jnp.concatenate(whole[: LANES // 8], axis=0).T
        rest = whole[LANES // 8 :] + [jnp.zeros((2 * LANES - SUMS, LANES), jnp.float32)]
        rest = jnp.concatenate(rest, axis=0).T

        def all_chunks(value):
            span = rows // 2
            while span >= side_z:
                value = value + pltpu.roll(value, span, 0)
                span //= 2
            return value

        for place, d in enumerate(group):
            main_rows = []
            for y in range(side_y):
                first = (place * side_y + y) * rows
                main_rows.append(all_chunks(main[first : first + rows]))
                value = all_chunks(rest[first : first + rows])
                spill = pltpu.roll(jnp.where(lane < SPILL, value, 0.0), SPILL_LANE + SPILL * d, 1)
                value = jnp.where(lane < SPILL, 0.0, value) + spill
                last[y] = value if last[y] is None else last[y] + value
            mine[ROW_OF[d]] = tiles_of(main_rows)
        if g < len(GROUPS) - 1:
            return
        pad = [jnp.zeros((rows, AFFINE_LANE), jnp.float32)]
        pad.append(jnp.concatenate([affine[y] for y in range(side_y)], axis=0))
        pad.append(jnp.zeros((rows, LANES - AFFINE_LANE - affine.shape[2]), jnp.float32))
        mine[DIRS] = tiles_of(last) + jnp.concatenate(pad, axis=1)

    def send(c, x, y, z, send_sem, recv_sem, other):
        first, end = CHUNKS[c]
        part = out.at[z, x, y, pl.ds(first, end - first)]
        return pltpu.make_async_remote_copy(
            src_ref=part,
            dst_ref=part,
            send_sem=send_sem,
            recv_sem=recv_sem,
            device_id=other,
            device_id_type=MESH,
        )

    def along(c, x, sign):
        other = (jnp.clip(at_x + sign, 0, count_x - 1), at_y, at_z)
        way = (sign + 1) // 2
        return send(c, x, at_y, at_z, line_send.at[c, way, x], line_recv.at[c, x], other)

    def direct(c, step):
        other = (jnp.clip(at_x + step, 0, count_x - 1), at_y, at_z)
        sem = direct_send.at[c, step + count_x - 1]
        return send(c, at_x, at_y, at_z, sem, line_recv.at[c, at_x], other)

    def across(c, x, way):
        other = (at_x, near_y[way], at_z)
        return send(c, x, at_y, at_z, side_send.at[c, way, x], side_recv.at[c, way, x], other)

    def across_in(c, x, way):
        other = (at_x, near_y[way], at_z)
        sems = side_send.at[c, way, x], side_recv.at[c, way, x]
        return send(c, x, near_y[way], at_z, *sems, other)

    def far_out(c, x, way):
        other = (at_x, near_y[1 - way], at_z)
        sems = side_send.at[c, 2, x], side_recv.at[c, 2, x]
        return send(c, x, near_y[way], at_z, *sems, other)

    def core_out(c, x, y, k):
        other = (at_x, at_y, (at_z + k) % count_z)
        sems = core_send.at[c, k - 1, x, y], core_recv.at[c, k - 1, x, y]
        return send(c, x, y, at_z, *sems, other)

    def core_in(c, x, y, k):
        from_z = (at_z + count_z - k) % count_z
        sems = core_send.at[c, k - 1, x, y], core_recv.at[c, k - 1, x, y]
        return send(c, x, y, from_z, *sems, (at_x, at_y, from_z))

    def to_cores(c, x, y):
        for k in range(1, count_z):
            core_out(c, x, y, k).start()

    def spread(c, x):
        for way in range(3 if FAR_DIRECT[c] else 2):
            across(c, x, way).start()
        to_cores(c, x, at_y)

    def own_out(c):
        for step in [k for far in range(count_x - 1, 0, -1) for k in (far, -far)]:
            if LINE_DIRECT[c] or abs(step) == 1:

                @pl.when((at_x + step >= 0) & (at_x + step < count_x))
                def _(step=step):
                    if LINE_DIRECT[c]:
                        direct(c, step).start()
                    else:
                        along(c, at_x, step).start()

        spread(c, at_x)

    def line_arrived(c, x, sign):
        along(c, x, sign).wait_recv()
        if not LINE_DIRECT[c]:

            @pl.when((at_x + sign >= 0) & (at_x + sign < count_x))
            def _():
                along(c, x, sign).start()

        spread(c, x)

    def side_arrived(c, x, sign):
        for way in range(2):
            across_in(c, x, way).wait_recv()
            if not FAR_DIRECT[c]:

                @pl.when(x % 2 == way)
                def _(way=way):
                    far_out(c, x, way).start()

            to_cores(c, x, near_y[way])

    def far_arrived(c, x, sign):
        across_in(c, x, 2).wait_recv()
        to_cores(c, x, near_y[2])

    def both_ways(c, distance, body):
        if distance == 0:
            body(c, at_x, 0)
        elif 0 < distance < count_x:

            @pl.when(at_x - distance >= 0)
            def _():
                body(c, at_x - distance, 1)

            @pl.when(at_x + distance < count_x)
            def _():
                body(c, at_x + distance, -1)

    def gather_round(c, r):
        if r == 0:
            own_out(c)
            return
        both_ways(c, r, line_arrived)
        both_ways(c, r - 1, side_arrived)
        both_ways(c, r - 2, far_arrived)

    rounds = count_x + 2
    done = [0] * len(GROUPS)

    def advance(c, many):
        for _ in range(many):
            if done[c] < rounds:
                gather_round(c, done[c])
                done[c] += 1

    for g in range(len(GROUPS)):
        here(g)
    for g in range(len(GROUPS)):
        for c, many in enumerate(ROUNDS_BEFORE[g]):
            advance(c, many)
        there_sums(g)
        advance(g, 1)
    while min(done) < rounds:
        for c in range(len(GROUPS)):
            if done[c] < rounds:
                advance(c, 1)

    solver = Solver(devices, bricks, blocks, turned_inverse)
    parts = out.reshape(out.shape[0] * count_x * count_y, DIRS + 1, 8, LANES)
    for c, (first, end) in enumerate(CHUNKS):

        def cores(i, carry, c=c):
            for k in range(1, count_z):
                core_in(c, i // count_y, i % count_y, k).wait_recv()
            return carry

        lax.fori_loop(0, count_x * count_y, cores, 0)
        for r in range(first, end):
            solver.load(parts, r)

    def sent(x, carry):
        for c in range(len(GROUPS)):
            for sign in (1, -1):
                if not LINE_DIRECT[c]:
                    passed = (at_x + sign >= 0) & (at_x + sign < count_x)
                    passed = passed & ((x <= at_x) if sign > 0 else (x >= at_x))

                    @pl.when(passed)
                    def _(sign=sign, c=c):
                        along(c, x, sign).wait_send()

            for way in range(3 if FAR_DIRECT[c] else 2):
                across(c, x, way).wait_send()
                if not FAR_DIRECT[c]:

                    @pl.when(x % 2 == way)
                    def _(way=way, c=c):
                        far_out(c, x, way).wait_send()

            def cores(y, inner, c=c):
                for k in range(1, count_z):
                    core_out(c, x, y, k).wait_send()
                return inner

            lax.fori_loop(0, count_y, cores, 0)
        return carry

    lax.fori_loop(0, count_x, sent, 0)
    for c in range(len(GROUPS)):
        for step in range(1 - count_x, count_x):
            if step and LINE_DIRECT[c]:

                @pl.when((at_x + step >= 0) & (at_x + step < count_x))
                def _(c=c, step=step):
                    direct(c, step).wait_send()

    for i, piece in enumerate(pieces):
        if any(piece[3]):

            @pl.when(in_mesh(piece[3]))
            def _(i=i):
                halo(i).wait_send()

    solver.run(anchor, update_out, residual_out, tiles)


def on_device(source_points, target_points, normals, weights, blocks, affines, anchor):
    bricks = source_points.shape[2:5]
    points = source_points.shape[5]
    devices = tuple(lax.axis_size(name) for name in AXES)
    grid = tuple(devices[axis] * bricks[axis] for axis in range(3))
    span = grid[0] * grid[1] * grid[2]
    chunks = points // LANES
    rows = chunks * bricks[2]
    assert bricks[0] == 1 and rows == 8 and devices[2] % 2 == 0 and devices[1] == 4
    assert bricks[1] * bricks[2] == 8
    assert span % (2 * LANES) == 0 and len(GROUPS[0]) * bricks[1] * rows == LANES

    def split(value):
        lead = value.shape[:-5]
        value = value.reshape(lead + (DIRS, bricks[1], bricks[2], chunks, LANES))
        return jnp.swapaxes(value, -3, -2)

    def filled(value):
        value = split(value)
        return value.reshape(value.shape[:-3] + (rows, LANES))

    params = functools.partial(pltpu.CompilerParams, vmem_limit_bytes=VMEM_BYTES)
    vmem = pl.BlockSpec(memory_space=pltpu.VMEM)
    smem = pl.BlockSpec(memory_space=pltpu.SMEM)
    anywhere = pl.BlockSpec(memory_space=pl.ANY)
    pieces = len(halo_pieces(bricks))
    dma = pltpu.SemaphoreType.DMA
    groups = len(GROUPS)
    own = (DIRS, bricks[1], rows, LANES)
    update, residual = pl.pallas_call(
        functools.partial(step_kernel, devices, bricks),
        out_shape=[jax.ShapeDtypeStruct(bricks[1:] + (12,), jnp.float32)] * 2,
        in_specs=[smem] + [anywhere] * 6,
        out_specs=[vmem, vmem],
        scratch_shapes=[
            pltpu.SMEM(bricks[1:] + (DIRS,), jnp.int32),
            pltpu.VMEM(bricks[1:] + (12,), jnp.float32),
            pltpu.VMEM(
                (devices[2], devices[0], devices[1], DIRS + 1, 8, LANES), jnp.float32
            ),
            pltpu.VMEM((DIRS + 1, LANES // 4, 8, span // 2), jnp.float32),
            pltpu.VMEM((36, 8, span // 2), jnp.float32),
            pltpu.VMEM((span // 2, LANES), jnp.float32),
            dma((2,)),
            pltpu.VMEM((3,) + own, jnp.float32),
            pltpu.VMEM((3,) + own, jnp.float32),
            pltpu.VMEM(own, jnp.float32),
            pltpu.VMEM((3, DIRS, bricks[1], chunks, bricks[2], LANES), jnp.float32),
            pltpu.VMEM((10, len(GROUPS), LANES, LANES), jnp.float32),
            pltpu.VMEM((len(GROUPS), SUMS, 8, LANES), jnp.float32),
            dma((3, DIRS)),
            dma((pieces,)),
            dma((pieces,)),
            dma((pieces,)),
            dma((groups, 2, devices[0])),
            dma((groups, 2 * devices[0] - 1)),
            dma((groups, devices[0])),
            dma((groups, 3, devices[0])),
            dma((groups, 3, devices[0])),
            dma((groups, devices[2] - 1, devices[0], devices[1])),
            dma((groups, devices[2] - 1, devices[0], devices[1])),
        ],
        compiler_params=params(collective_id=0, has_side_effects=True),
        name="step",
    )(
        anchor,
        jnp.transpose(blocks, (1, 2, 3, 0)).reshape(bricks[1], bricks[2], DIRS),
        jnp.transpose(affines, (1, 2, 3, 0)).reshape(bricks[1], bricks[2], 12),
        filled(source_points),
        split(target_points),
        filled(normals),
        filled(weights),
    )
    def placed(value):
        return jnp.transpose(value, (2, 0, 1)).reshape((12,) + bricks)

    return placed(update), placed(residual)


def solution(mesh):
    points = P(None, None, "gx", "gy", "gz", None)
    tiles = P(None, "gx", "gy", "gz")
    return jax.shard_map(
        on_device,
        mesh=mesh,
        in_specs=(points, points, points, P(None, "gx", "gy", "gz", None), tiles, tiles, P()),
        out_specs=(tiles, tiles),
        check_vma=False,
    )
```

time: 47 us -> 44.3 us (0.943)
  Pallas kernels: 45.5 us -> 40.8 us
  local copies, waits for them, and re-layouts: 0 us -> 1.94 us
    pallas_call x2 -> x1, Pallas kernels: 45.5 us -> 40.8 us  [on_device(): pl.pallas_call(functools.partial(step_kernel, devices, bricks), out_shape...]
    unnamed x0 -> x6, local copies, waits for them, and re-layouts: none -> 1.94 us
where the time goes in v2:
time: 44.3 us; the launch traced here: 44.1 us
  Pallas kernels  40.8 us (92%)
  local copies, waits for them, and re-layouts  1.94 us (4%)
  between operations  1.3 us (3%)
    pallas_call x1, Pallas kernels, on_device(): pl.pallas_call(functools.partial(step_kernel, devices, bricks), out_shape...  40.8 us
    unnamed x6, local copies, waits for them, and re-layouts  1.94 us

profile of v2, /device:TPU:0, one launch (start us, length us, event | category | flops | bytes accessed | tf_op | source)
XLA Modules:
  0.0 44.1 jit_solution(4291073605815561686)
XLA Ops:
  1.3 40.8 %step.1 = (f32[4,2,12]{2,1,0:T(2,128)}, f32[4,2,12]{2,1,0:T(2,128)}) custom-call(s32[1]{0:T(128)S(6)} %copy.20.anchor, s32[4,2,13]{2,1,0:T(2,128)} %bitcast.34, f32[4,2,12]{2,1,0:T(2,128)} %bitcast.35, f32[3,13,4,8,128]{4,3,2,1,0:T(8,128)} %bitcast.30, f32[3,13,4,4,2,128]{5,4,3,2,1,0:T(2,128)} %bitcast.31, f32[3,13,4,8,128]{4,3,2,1,0:T(8,128)} %bitcast.32, ...), custom_call_target="tpu_custom_call" | custom-call | tf_op jit(solution)/shard_map/step/pallas_call | solution.py:795
  42.1 0.0 copy-start.1
  42.1 0.7 %copy-done.1 = f32[4,2,12]{2,1,0:T(2,128)S(1)} copy-done((f32[4,2,12]{2,1,0:T(2,128)S(1)}, f32[4,2,12]{2,1,0:T(2,128)}, u32[]{:S(2)}) %copy-start.1) | copy-done | bytes 408
  42.8 0.0 copy-start
  42.8 0.6 %copy.21 = f32[12,1,4,2]{0,3,2,1:T(2,128)} copy(f32[12,1,4,2]{0,3,2,1:T(2,128)S(1)} %bitcast.37) | data formatting | bytes 768
  43.4 0.1 copy-done
  43.5 0.6 %copy.22 = f32[12,1,4,2]{0,3,2,1:T(2,128)} copy(f32[12,1,4,2]{0,3,2,1:T(2,128)S(1)} %bitcast.36) | data formatting | bytes 768
Async XLA Ops:
  42.1 0.7 %copy-start.1 = (f32[4,2,12]{2,1,0:T(2,128)S(1)}, f32[4,2,12]{2,1,0:T(2,128)}, u32[]{:S(2)}) copy-start(f32[4,2,12]{2,1,0:T(2,128)} %get-tuple-element.4) | copy-start | bytes 1156
  42.8 0.7 %copy-start = (f32[4,2,12]{2,1,0:T(2,128)S(1)}, f32[4,2,12]{2,1,0:T(2,128)}, u32[]{:S(2)}) copy-start(f32[4,2,12]{2,1,0:T(2,128)} %get-tuple-element.5) | copy-start | bytes 1156

commit v3 on v2

--- a/solution.py
+++ b/solution.py
@@ -40,14 +40,18 @@
 SUMS = PAIR_ROWS + 2 * THERE_ROWS
 SPILL_LANE = SPILL + THERE_ROWS
 AFFINE_LANE = SPILL_LANE + SPILL * DIRS
-SEND_ORDER = (3, 4, 5, 9, 7, 12, 0, 6, 10, 8, 11, 1, 2)
+SEND_ORDER = (1, 2, 8, 11, 3, 4, 9, 5, 7, 0, 6, 12, 10)
 GROUPS = ((1, 2, 8, 11), (3, 4, 5, 9), (7, 12, 0, 6), (10,))
 ROW_OF = {d: place for place, d in enumerate(d for group in GROUPS for d in group)}
 DIRECTION_OF = {place: d for d, place in ROW_OF.items()}
 CHUNKS = ((0, 4), (4, 8), (8, 12), (12, DIRS + 1))
-LINE_DIRECT = (True, True, True, True)
-FAR_DIRECT = (True, True, True, True)
-ROUNDS_BEFORE = ((), (0,), (0, 0), (0, 0, 0))
+DIRECT = (0, 1, 2, 3)
+SCHEDULE = (
+    "here 0", "here 1", "here 2", "here 3", "there 0", "line 0", "there 1", "line 1",
+    "there 2", "line 2", "side 0", "there 3", "line 3", "side 1", "side 2", "far 0", "side 3",
+    "far 1", "core 0", "far 2", "core 1", "load 0", "far 3", "core 2", "load 1", "core 3",
+    "load 2", "load 3",
+)
 
 
 def normal_pair(c, k):
@@ -108,11 +112,11 @@
                     [first[4 * i : 4 * i + 4], second[4 * i : 4 * i + 4]], axis=0
                 )
 
-    def run(self, anchor, update_out, residual_out, tiles):
-        solve(self.grid, self.bricks, anchor, update_out, residual_out, self.blocks, self.turned, tiles)
-
-
-def solve(grid, bricks, anchor, update_out, residual_out, blocks, turned, tiles):
+    def run(self, anchor, result_out, tiles):
+        solve(self.grid, self.bricks, anchor, result_out, self.blocks, self.turned, tiles)
+
+
+def solve(grid, bricks, anchor, result_out, blocks, turned, tiles):
     count_x, count_y, count_z = grid
     _, side_y, side_z = bricks
     half = blocks.shape[3]
@@ -284,7 +288,11 @@
         ]
 
     def dot(left, right):
-        return jnp.sum(total(left[k] * right[k] for k in range(3)), keepdims=True)
+        value = total(left[k] * right[k] for k in range(3))
+        value = total(value[:, start : start + LANES] for start in range(0, half, LANES))
+        for span in (4, 2, 1):
+            value = value + pltpu.roll(value, span, 0)
+        return jnp.sum(value, axis=1, keepdims=True)
 
     first = precondition(rhs)
 
@@ -315,24 +323,25 @@
     rows = tiles[pl.ds(pl.multiple_of(base, 8), side_y * side_z), :]
     for y in range(side_y):
         row = rows[y * side_z : (y + 1) * side_z]
-        update_out[y] = row[:, :12]
-        residual_out[y] = row[:, 12:24]
+        result_out[y] = row[:, :24]
 
 
 def step_kernel(
     devices, bricks,
-    anchor, count_in, affine_in, source, target, normal, weight,
-    update_out, residual_out,
-    count, affine, out, blocks, turned_inverse, tiles, small_sem,
+    anchor_in, count_in, affine_in, source, target, normal, weight,
+    result_out,
+    anchor, count, affine, out, blocks, turned_inverse, tiles, small_sem,
     own_p, own_n, own_w, there, turned, acc,
     load_sem, stay_sem, halo_send, halo_recv,
-    line_send, direct_send, line_recv, side_send, side_recv, core_send, core_recv,
+    line_send, line_recv, side_send, side_recv, core_send, core_recv,
 ):
     count_x, count_y, count_z = devices
     _, side_y, side_z = bricks
     at = tuple(lax.axis_index(name) for name in AXES)
     at_x, at_y, at_z = at
     pieces = halo_pieces(bricks)
+    leaving = [i for i, piece in enumerate(pieces) if any(piece[3])]
+    staying = [i for i, piece in enumerate(pieces) if not any(piece[3])]
     chunks = source.shape[3] // side_z
 
     def in_mesh(offset):
@@ -356,23 +365,18 @@
     small = (
         pltpu.make_async_copy(count_in, count, small_sem.at[0]),
         pltpu.make_async_copy(affine_in, affine, small_sem.at[1]),
+        pltpu.make_async_copy(anchor_in, anchor, small_sem.at[2]),
     )
     for copy in small:
         copy.start()
 
-    loads = []
-    for g, group in enumerate(GROUPS):
-        for d in group:
-            loads.append(
-                (
-                    pltpu.make_async_copy(source.at[:, d], own_p.at[:, d], load_sem.at[0, d]),
-                    pltpu.make_async_copy(normal.at[:, d], own_n.at[:, d], load_sem.at[1, d]),
-                    pltpu.make_async_copy(weight.at[d], own_w.at[d], load_sem.at[2, d]),
-                )
-            )
-            for copy in loads[-1]:
-                copy.start()
-    loads = dict(zip([d for group in GROUPS for d in group], loads))
+    loads = (
+        pltpu.make_async_copy(source, own_p, load_sem.at[0]),
+        pltpu.make_async_copy(normal, own_n, load_sem.at[1]),
+        pltpu.make_async_copy(weight, own_w, load_sem.at[2]),
+    )
+    for copy in loads:
+        copy.start()
 
     zeros = jnp.zeros(there.shape[2:], jnp.float32)
     for c in range(3):
@@ -409,15 +413,15 @@
         return pltpu.make_async_remote_copy(
             src_ref=spot(target, d, start),
             dst_ref=spot(there, d, end),
-            send_sem=halo_send.at[i],
-            recv_sem=halo_recv.at[i],
+            send_sem=halo_send.at[leaving.index(i)],
+            recv_sem=halo_recv.at[leaving.index(i)],
             device_id=beside(step),
             device_id_type=MESH,
         )
 
     def stay(i):
         d, start, end, _ = pieces[i]
-        return pltpu.make_async_copy(spot(target, d, start), spot(there, d, end), stay_sem.at[i])
+        return pltpu.make_async_copy(spot(target, d, start), spot(there, d, end), stay_sem.at[staying.index(i)])
 
     for i, piece in enumerate(pieces):
         if any(piece[3]):
@@ -506,8 +510,8 @@
 
     def here(g):
         group = GROUPS[g]
-        for d in group:
-            for copy in loads[d]:
+        if g == 0:
+            for copy in loads:
                 copy.wait()
         for c in range(3):
             turned[c, g] = turn([own_p[c, d, y] for d in group for y in range(side_y)])
@@ -569,6 +573,9 @@
         pad.append(jnp.zeros((rows, LANES - AFFINE_LANE - affine.shape[2]), jnp.float32))
         mine[DIRS] = tiles_of(last) + jnp.concatenate(pad, axis=1)
 
+    everyone = pl.ds(0, count_x)
+    halves = (pl.ds(0, count_x // 2), pl.ds(count_x // 2, count_x - count_x // 2))
+
     def send(c, x, y, z, send_sem, recv_sem, other):
         first, end = CHUNKS[c]
         part = out.at[z, x, y, pl.ds(first, end - first)]
@@ -581,178 +588,121 @@
             device_id_type=MESH,
         )
 
-    def along(c, x, sign):
-        other = (jnp.clip(at_x + sign, 0, count_x - 1), at_y, at_z)
-        way = (sign + 1) // 2
-        return send(c, x, at_y, at_z, line_send.at[c, way, x], line_recv.at[c, x], other)
-
-    def direct(c, step):
+    def along(c, step):
         other = (jnp.clip(at_x + step, 0, count_x - 1), at_y, at_z)
-        sem = direct_send.at[c, step + count_x - 1]
-        return send(c, at_x, at_y, at_z, sem, line_recv.at[c, at_x], other)
+        return send(c, at_x, at_y, at_z, line_send.at[c], line_recv.at[c, at_x], other)
+
+    def along_in(c, x):
+        return send(c, x, at_y, at_z, line_send.at[c], line_recv.at[c, x], (x, at_y, at_z))
+
+    def along_sent(c):
+        x = pl.ds(0, count_x - 1)
+        return send(c, x, at_y, at_z, line_send.at[c], line_recv.at[c, 0], (at_x, at_y, at_z))
 
     def across(c, x, way):
         other = (at_x, near_y[way], at_z)
-        return send(c, x, at_y, at_z, side_send.at[c, way, x], side_recv.at[c, way, x], other)
-
-    def across_in(c, x, way):
+        return send(c, x, at_y, at_z, side_send.at[c, way], side_recv.at[c, way], other)
+
+    def across_in(c, way):
         other = (at_x, near_y[way], at_z)
-        sems = side_send.at[c, way, x], side_recv.at[c, way, x]
-        return send(c, x, near_y[way], at_z, *sems, other)
-
-    def far_out(c, x, way):
+        return send(c, everyone, near_y[way], at_z, side_send.at[c, way], side_recv.at[c, way], other)
+
+    def relay(c, way):
         other = (at_x, near_y[1 - way], at_z)
-        sems = side_send.at[c, 2, x], side_recv.at[c, 2, x]
-        return send(c, x, near_y[way], at_z, *sems, other)
+        sems = side_send.at[c, 2 + way], side_recv.at[c, 2 + way]
+        return send(c, halves[way], near_y[way], at_z, *sems, other)
+
+    def relay_in(c, way):
+        other = (at_x, near_y[1 - way], at_z)
+        sems = side_send.at[c, 2 + way], side_recv.at[c, 2 + way]
+        return send(c, halves[way], near_y[2], at_z, *sems, other)
 
     def core_out(c, x, y, k):
         other = (at_x, at_y, (at_z + k) % count_z)
-        sems = core_send.at[c, k - 1, x, y], core_recv.at[c, k - 1, x, y]
-        return send(c, x, y, at_z, *sems, other)
-
-    def core_in(c, x, y, k):
-        from_z = (at_z + count_z - k) % count_z
-        sems = core_send.at[c, k - 1, x, y], core_recv.at[c, k - 1, x, y]
-        return send(c, x, y, from_z, *sems, (at_x, at_y, from_z))
+        return send(c, x, y, at_z, core_send.at[c, k - 1], core_recv.at[c, k - 1], other)
+
+    def core_all(c, z, k):
+        other = (at_x, at_y, (at_z + k) % count_z)
+        every_y = pl.ds(0, count_y)
+        return send(c, everyone, every_y, z, core_send.at[c, k - 1], core_recv.at[c, k - 1], other)
 
     def to_cores(c, x, y):
         for k in range(1, count_z):
             core_out(c, x, y, k).start()
 
     def spread(c, x):
-        for way in range(3 if FAR_DIRECT[c] else 2):
+        for way in (2, 0, 1) if c in DIRECT else (0, 1):
             across(c, x, way).start()
         to_cores(c, x, at_y)
 
-    def own_out(c):
-        for step in [k for far in range(count_x - 1, 0, -1) for k in (far, -far)]:
-            if LINE_DIRECT[c] or abs(step) == 1:
-
-                @pl.when((at_x + step >= 0) & (at_x + step < count_x))
-                def _(step=step):
-                    if LINE_DIRECT[c]:
-                        direct(c, step).start()
-                    else:
-                        along(c, at_x, step).start()
+    far_first = [k for far in range(count_x - 1, 0, -1) for k in (far, -far)]
+
+    def others(body):
+        for step in far_first[::-1]:
+
+            @pl.when((at_x + step >= 0) & (at_x + step < count_x))
+            def _(step=step):
+                body(step)
+
+    def line(c):
+        for step in far_first:
+
+            @pl.when((at_x + step >= 0) & (at_x + step < count_x))
+            def _(step=step):
+                along(c, step).start()
 
         spread(c, at_x)
 
-    def line_arrived(c, x, sign):
-        along(c, x, sign).wait_recv()
-        if not LINE_DIRECT[c]:
-
-            @pl.when((at_x + sign >= 0) & (at_x + sign < count_x))
-            def _():
-                along(c, x, sign).start()
-
-        spread(c, x)
-
-    def side_arrived(c, x, sign):
+    def side(c):
+        def body(step):
+            along_in(c, at_x + step).wait_recv()
+            spread(c, at_x + step)
+
+        others(body)
+
+    def far(c):
         for way in range(2):
-            across_in(c, x, way).wait_recv()
-            if not FAR_DIRECT[c]:
-
-                @pl.when(x % 2 == way)
-                def _(way=way):
-                    far_out(c, x, way).start()
-
-            to_cores(c, x, near_y[way])
-
-    def far_arrived(c, x, sign):
-        across_in(c, x, 2).wait_recv()
-        to_cores(c, x, near_y[2])
-
-    def both_ways(c, distance, body):
-        if distance == 0:
-            body(c, at_x, 0)
-        elif 0 < distance < count_x:
-
-            @pl.when(at_x - distance >= 0)
-            def _():
-                body(c, at_x - distance, 1)
-
-            @pl.when(at_x + distance < count_x)
-            def _():
-                body(c, at_x + distance, -1)
-
-    def gather_round(c, r):
-        if r == 0:
-            own_out(c)
-            return
-        both_ways(c, r, line_arrived)
-        both_ways(c, r - 1, side_arrived)
-        both_ways(c, r - 2, far_arrived)
-
-    rounds = count_x + 2
-    done = [0] * len(GROUPS)
-
-    def advance(c, many):
-        for _ in range(many):
-            if done[c] < rounds:
-                gather_round(c, done[c])
-                done[c] += 1
-
-    for g in range(len(GROUPS)):
-        here(g)
-    for g in range(len(GROUPS)):
-        for c, many in enumerate(ROUNDS_BEFORE[g]):
-            advance(c, many)
-        there_sums(g)
-        advance(g, 1)
-    while min(done) < rounds:
-        for c in range(len(GROUPS)):
-            if done[c] < rounds:
-                advance(c, 1)
+            across_in(c, way).wait_recv()
+            if c not in DIRECT:
+                relay(c, way).start()
+            to_cores(c, everyone, near_y[way])
+
+    def core(c):
+        if c in DIRECT:
+            across_in(c, 2).wait_recv()
+        else:
+            for way in range(2):
+                relay_in(c, way).wait_recv()
+        to_cores(c, everyone, near_y[2])
 
     solver = Solver(devices, bricks, blocks, turned_inverse)
-    parts = out.reshape(out.shape[0] * count_x * count_y, DIRS + 1, 8, LANES)
-    for c, (first, end) in enumerate(CHUNKS):
-
-        def cores(i, carry, c=c):
-            for k in range(1, count_z):
-                core_in(c, i // count_y, i % count_y, k).wait_recv()
-            return carry
-
-        lax.fori_loop(0, count_x * count_y, cores, 0)
-        for r in range(first, end):
+    parts = out.reshape(count_z * count_x * count_y, DIRS + 1, 8, LANES)
+
+    def load(c):
+        for k in range(1, count_z):
+            core_all(c, (at_z + count_z - k) % count_z, k).wait_recv()
+        for r in range(*CHUNKS[c]):
             solver.load(parts, r)
 
-    def sent(x, carry):
-        for c in range(len(GROUPS)):
-            for sign in (1, -1):
-                if not LINE_DIRECT[c]:
-                    passed = (at_x + sign >= 0) & (at_x + sign < count_x)
-                    passed = passed & ((x <= at_x) if sign > 0 else (x >= at_x))
-
-                    @pl.when(passed)
-                    def _(sign=sign, c=c):
-                        along(c, x, sign).wait_send()
-
-            for way in range(3 if FAR_DIRECT[c] else 2):
-                across(c, x, way).wait_send()
-                if not FAR_DIRECT[c]:
-
-                    @pl.when(x % 2 == way)
-                    def _(way=way, c=c):
-                        far_out(c, x, way).wait_send()
-
-            def cores(y, inner, c=c):
-                for k in range(1, count_z):
-                    core_out(c, x, y, k).wait_send()
-                return inner
-
-            lax.fori_loop(0, count_y, cores, 0)
-        return carry
-
-    lax.fori_loop(0, count_x, sent, 0)
-    for c in range(len(GROUPS)):
-        for step in range(1 - count_x, count_x):
-            if step and LINE_DIRECT[c]:
-
-                @pl.when((at_x + step >= 0) & (at_x + step < count_x))
-                def _(c=c, step=step):
-                    direct(c, step).wait_send()
-
+    actions = {
+        "here": here, "there": there_sums, "line": line, "side": side, "far": far, "core": core,
+        "load": load,
+    }
+    for entry in SCHEDULE:
+        name, g = entry.split()
+        actions[name](int(g))
+
+    for c in range(len(CHUNKS)):
+        along_sent(c).wait_send()
+        for way in range(2):
+            across_in(c, way).wait_send()
+        if c in DIRECT:
+            across_in(c, 2).wait_send()
+        else:
+            for way in range(2):
+                relay(c, way).wait_send()
+        for k in range(1, count_z):
+            core_all(c, at_z, k).wait_send()
     for i, piece in enumerate(pieces):
         if any(piece[3]):
 
@@ -760,7 +710,7 @@
             def _(i=i):
                 halo(i).wait_send()
 
-    solver.run(anchor, update_out, residual_out, tiles)
+    solver.run(anchor, result_out, tiles)
 
 
 def on_device(source_points, target_points, normals, weights, blocks, affines, anchor):
@@ -786,18 +736,19 @@
 
     params = functools.partial(pltpu.CompilerParams, vmem_limit_bytes=VMEM_BYTES)
     vmem = pl.BlockSpec(memory_space=pltpu.VMEM)
-    smem = pl.BlockSpec(memory_space=pltpu.SMEM)
     anywhere = pl.BlockSpec(memory_space=pl.ANY)
-    pieces = len(halo_pieces(bricks))
+    pieces = halo_pieces(bricks)
+    remote = sum(any(piece[3]) for piece in pieces)
     dma = pltpu.SemaphoreType.DMA
     groups = len(GROUPS)
     own = (DIRS, bricks[1], rows, LANES)
-    update, residual = pl.pallas_call(
+    result = pl.pallas_call(
         functools.partial(step_kernel, devices, bricks),
-        out_shape=[jax.ShapeDtypeStruct(bricks[1:] + (12,), jnp.float32)] * 2,
-        in_specs=[smem] + [anywhere] * 6,
-        out_specs=[vmem, vmem],
+        out_shape=jax.ShapeDtypeStruct(bricks[1:] + (24,), jnp.float32),
+        in_specs=[anywhere] * 7,
+        out_specs=vmem,
         scratch_shapes=[
+            pltpu.SMEM((1,), jnp.int32),
             pltpu.SMEM(bricks[1:] + (DIRS,), jnp.int32),
             pltpu.VMEM(bricks[1:] + (12,), jnp.float32),
             pltpu.VMEM(
@@ -806,24 +757,23 @@
             pltpu.VMEM((DIRS + 1, LANES // 4, 8, span // 2), jnp.float32),
             pltpu.VMEM((36, 8, span // 2), jnp.float32),
             pltpu.VMEM((span // 2, LANES), jnp.float32),
-            dma((2,)),
+            dma((3,)),
             pltpu.VMEM((3,) + own, jnp.float32),
             pltpu.VMEM((3,) + own, jnp.float32),
             pltpu.VMEM(own, jnp.float32),
             pltpu.VMEM((3, DIRS, bricks[1], chunks, bricks[2], LANES), jnp.float32),
             pltpu.VMEM((10, len(GROUPS), LANES, LANES), jnp.float32),
             pltpu.VMEM((len(GROUPS), SUMS, 8, LANES), jnp.float32),
-            dma((3, DIRS)),
-            dma((pieces,)),
-            dma((pieces,)),
-            dma((pieces,)),
-            dma((groups, 2, devices[0])),
-            dma((groups, 2 * devices[0] - 1)),
+            dma((3,)),
+            dma((len(pieces) - remote,)),
+            dma((remote,)),
+            dma((remote,)),
+            dma((groups,)),
             dma((groups, devices[0])),
-            dma((groups, 3, devices[0])),
-            dma((groups, 3, devices[0])),
-            dma((groups, devices[2] - 1, devices[0], devices[1])),
-            dma((groups, devices[2] - 1, devices[0], devices[1])),
+            dma((groups, 4)),
+            dma((groups, 4)),
+            dma((groups, devices[2] - 1)),
+            dma((groups, devices[2] - 1)),
         ],
         compiler_params=params(collective_id=0, has_side_effects=True),
         name="step",
@@ -839,7 +789,7 @@
     def placed(value):
         return jnp.transpose(value, (2, 0, 1)).reshape((12,) + bricks)
 
-    return placed(update), placed(residual)
+    return placed(result[..., :12]), placed(result[..., 12:])
 
 
 def solution(mesh):

time: 44.3 us -> 37.5 us (0.85)
  Pallas kernels: 40.8 us -> 34.6 us
  local copies, waits for them, and re-layouts: 1.94 us -> 1.41 us
    pallas_call x1, Pallas kernels: 40.8 us -> 34.6 us  [on_device(): pl.pallas_call(functools.partial(step_kernel, devices, bricks), out_shape...]
    unnamed x6 -> x0, local copies, waits for them, and re-layouts: 1.94 us -> none
    reshape x0 -> x1, local copies, waits for them, and re-layouts: none -> 1.41 us  [placed(): return jnp.transpose(value, (2, 0, 1)).reshape((12,) + bricks)]
where the time goes in v3:
time: 37.5 us; the launch traced here: 37.3 us
  Pallas kernels  34.6 us (92%)
  local copies, waits for them, and re-layouts  1.41 us (4%)
  between operations  1.29 us (3%)
    pallas_call x1, Pallas kernels, on_device(): pl.pallas_call(functools.partial(step_kernel, devices, bricks), out_shape...  34.6 us
    reshape x1, local copies, waits for them, and re-layouts, placed(): return jnp.transpose(value, (2, 0, 1)).reshape((12,) + bricks)  1.41 us

profile of v3, /device:TPU:0, one launch (start us, length us, event | category | flops | bytes accessed | tf_op | source)
XLA Modules:
  0.0 37.3 jit_solution(10830639706253957901)
XLA Ops:
  1.3 34.6 %step.1 = f32[4,2,24]{2,1,0:T(2,128)} custom-call(s32[1]{0:T(128)S(6)} %copy.18.anchor_in, s32[4,2,13]{2,1,0:T(2,128)} %bitcast.36, f32[4,2,12]{2,1,0:T(2,128)} %bitcast.37, f32[3,13,4,8,128]{4,3,2,1,0:T(8,128)} %bitcast.32, f32[3,13,4,4,2,128]{5,4,3,2,1,0:T(2,128)} %bitcast.33, f32[3,13,4,8,128]{4,3,2,1,0:T(8,128)} %bitcast.34, f32[13,4,8,128]{3,2,1,0:T(8,128)} %bitcast.35), custom_call_target="tpu_custom_call" | custom-call | tf_op jit(solution)/shard_map/step/pallas_call | solution.py:745
  35.9 1.4 %slice_bitcast_fusion = (f32[12,1,4,2]{0,3,2,1:T(2,128)}, f32[12,1,4,2]{0,3,2,1:T(2,128)}) fusion(f32[4,2,24]{2,1,0:T(2,128)} %step.1), kind=kLoop, calls=%fused_computation | loop fusion | bytes 1536 | tf_op jit(solution)/shard_map/reshape | solution.py:790

commit v4 on v3

--- a/solution.py
+++ b/solution.py
@@ -40,17 +40,21 @@
 SUMS = PAIR_ROWS + 2 * THERE_ROWS
 SPILL_LANE = SPILL + THERE_ROWS
 AFFINE_LANE = SPILL_LANE + SPILL * DIRS
-SEND_ORDER = (1, 2, 8, 11, 3, 4, 9, 5, 7, 0, 6, 12, 10)
-GROUPS = ((1, 2, 8, 11), (3, 4, 5, 9), (7, 12, 0, 6), (10,))
+SEND_ORDER = (1, 2, 8, 11, 3, 4, 9, 5, 7, 6, 12, 10)
+GROUPS = ((1, 2, 8, 11), (3, 4, 5, 9), (7, 12, 6), (10, 0))
+FLIPPED = 0
+PLACED = tuple(tuple(-part for part in o) if d == FLIPPED else o for d, o in enumerate(OFFSETS))
 ROW_OF = {d: place for place, d in enumerate(d for group in GROUPS for d in group)}
 DIRECTION_OF = {place: d for d, place in ROW_OF.items()}
-CHUNKS = ((0, 4), (4, 8), (8, 12), (12, DIRS + 1))
+CHUNKS = ((0, 4), (4, 8), (8, 11), (11, DIRS + 1))
 DIRECT = (0, 1, 2, 3)
+LATE = (10,)
 SCHEDULE = (
-    "here 0", "here 1", "here 2", "here 3", "there 0", "line 0", "there 1", "line 1",
-    "there 2", "line 2", "side 0", "there 3", "line 3", "side 1", "side 2", "far 0", "side 3",
-    "far 1", "core 0", "far 2", "core 1", "load 0", "far 3", "core 2", "load 1", "core 3",
-    "load 2", "load 3",
+    "here 0", "here 1", "here 2", "there 0", "line 0", "late", "there 1",
+    "line 1", "side 0", "there 2", "line 2", "here 3", "side 1", "there 3",
+    "line 3", "side 2", "side 3", "far 0", "far 1", "core 0", "far 2",
+    "core 1", "load 0", "far 3", "core 2", "load 1", "core 3", "load 2",
+    "load 3",
 )
 
 
@@ -163,38 +167,43 @@
             ]
         return terms[0]
 
-    def transposed(d, spreads):
-        return [
-            total(
-                blocks[d, normal_pair(c, k) * 4 + e] * spreads[c][e]
-                for c in range(3)
-                for e in range(4)
-            )
-            for k in range(3)
+    JOINED = ((0, 1), (0, 2), (1, 2))
+
+    def joins(vector):
+        return [vector[c] + vector[k] for c, k in JOINED]
+
+    def symmetric(d, e, vector, joined):
+        shared = [
+            blocks[d, normal_pair(*pair) * 4 + e] * value for pair, value in zip(JOINED, joined)
         ]
+        own = [blocks[d, normal_pair(k, k) * 4 + e] * vector[k] for k in range(3)]
+        return [own[k] + (shared[(0, 0, 1)[k]] + shared[(1, 2, 2)[k]]) for k in range(3)]
+
+    def transposed(d, columns):
+        rows = [symmetric(d, e, *columns[e]) for e in range(4)]
+        return [total(rows[e][k] for e in range(4)) for k in range(3)]
 
     def operate(vector, shifted=False):
-        spreads = [[spread(vector[c], e) for e in range(4)] for c in range(3)]
-        result = transposed(DIRS, spreads)
+        columns = [[spread(vector[c], e) for c in range(3)] for e in range(4)]
+        columns = [(column_e, joins(column_e)) for column_e in columns]
+        result = transposed(DIRS, columns)
         sums = [[None] * 4 for _ in range(3)]
         back = [None] * 3
-        for d, offset in enumerate(OFFSETS):
+        for d, offset in enumerate(PLACED):
             near = [ahead(vector[k], offset) for k in range(3)]
-            here = spreads
+            here = columns
             if shifted:
                 near = [
                     near[k] + jnp.where(column == 3, SPACING * offset[k], 0.0) for k in range(3)
                 ]
-                here = [
-                    spreads[c][:3] + [spreads[c][3] - SPACING * offset[c]] for c in range(3)
-                ]
+                edge = [columns[3][0][c] - SPACING * offset[c] for c in range(3)]
+                here = columns[:3] + [(edge, joins(edge))]
             sent = transposed(d, here)
-            for c in range(3):
-                for e in range(4):
-                    term = total(
-                        blocks[d, normal_pair(c, k) * 4 + e] * near[k] for k in range(3)
-                    )
-                    sums[c][e] = term if sums[c][e] is None else sums[c][e] + term
+            joined = joins(near)
+            for e in range(4):
+                terms = symmetric(d, e, near, joined)
+                for c in range(3):
+                    sums[c][e] = terms[c] if sums[c][e] is None else sums[c][e] + terms[c]
             for k in range(3):
                 term = ahead(sent[k], offset, -1)
                 back[k] = term if back[k] is None else back[k] + term
@@ -206,7 +215,7 @@
     both = []
     for g in range(THERE_ROWS // 4):
         value = blocks[DIRS, SPILL // 4 + g]
-        for d, offset in enumerate(OFFSETS):
+        for d, offset in enumerate(PLACED):
             group = PAIR_ROWS // 4 + g
             if group < LANES // 4:
                 term = blocks[d, group]
@@ -219,7 +228,7 @@
     diagonal = []
     for s in range(6):
         edge = None
-        for d, offset in enumerate(OFFSETS):
+        for d, offset in enumerate(PLACED):
             term = ahead(blocks[d, s * 4 + 3], offset, -1)
             edge = term if edge is None else edge + term
         for e in range(4):
@@ -232,20 +241,15 @@
                 value = jnp.where(column == f, spread(both[i // 4], i % 4), value)
             diagonal.append(value)
         diagonal.append(edge)
-    for i, value in enumerate(diagonal):
-        blocks[DIRS, i] = value
-
     brick_z = lane // plane + jnp.where(low, 0, half // plane)
     flat = lane % plane // side_z * count_z + brick_z * side_z + lane % side_z
     keep = (flat != anchor[0]).astype(jnp.float32)
-    rhs = [-(keep * value) for value in operate(affine, True)]
-
     matrix = []
     for c in range(3):
         for e in range(4):
             row = []
             for k in range(3):
-                value = blocks[DIRS, normal_pair(c, k) * 4 + e]
+                value = diagonal[normal_pair(c, k) * 4 + e]
                 if c == k:
                     eye = (column == e).astype(jnp.float32)
                     damped = value + DAMPING * eye
@@ -254,6 +258,20 @@
                     blocks_value = keep * value
                 row.append(blocks_value)
             matrix.append(row)
+    for i, value in enumerate(diagonal):
+        blocks[DIRS, i] = value
+
+    def reduce_own(d):
+        for e in range(4):
+            shared = [blocks[d, normal_pair(*pair) * 4 + e] for pair in JOINED]
+            for k in range(3):
+                own = normal_pair(k, k) * 4 + e
+                both_shared = shared[(0, 0, 1)[k]] + shared[(1, 2, 2)[k]]
+                blocks[d, own] = blocks[d, own] - both_shared
+
+    for d in range(DIRS + 1):
+        reduce_own(d)
+    rhs = [-(keep * value) for value in operate(affine, True)]
     for s, (c, k) in enumerate(NORMAL_PAIRS):
         if c == k:
             for e in range(4):
@@ -331,9 +349,9 @@
     anchor_in, count_in, affine_in, source, target, normal, weight,
     result_out,
     anchor, count, affine, out, blocks, turned_inverse, tiles, small_sem,
-    own_p, own_n, own_w, there, turned, acc,
+    own_q, own_p, own_n, own_w, sent_w, flip_p, flip_n, flip_w, there, turned, acc,
     load_sem, stay_sem, halo_send, halo_recv,
-    line_send, line_recv, side_send, side_recv, core_send, core_recv,
+    flip_send, flip_recv, sent, line_recv, side_recv, core_recv,
 ):
     count_x, count_y, count_z = devices
     _, side_y, side_z = bricks
@@ -370,6 +388,8 @@
     for copy in small:
         copy.start()
 
+    load_target = pltpu.make_async_copy(target, own_q, load_sem.at[3])
+    load_target.start()
     loads = (
         pltpu.make_async_copy(source, own_p, load_sem.at[0]),
         pltpu.make_async_copy(normal, own_n, load_sem.at[1]),
@@ -378,10 +398,14 @@
     for copy in loads:
         copy.start()
 
+    for ref in (flip_p, flip_n, flip_w):
+        ref[...] = jnp.zeros_like(ref)
     zeros = jnp.zeros(there.shape[2:], jnp.float32)
     for c in range(3):
         for d in range(DIRS):
             there[c, d] = zeros
+
+    acc[...] = jnp.zeros_like(acc)
 
     barrier = pltpu.get_barrier_semaphore()
     steps = {piece[3] for piece in pieces if any(piece[3])}
@@ -411,7 +435,7 @@
     def halo(i):
         d, start, end, step = pieces[i]
         return pltpu.make_async_remote_copy(
-            src_ref=spot(target, d, start),
+            src_ref=spot(own_q, d, start),
             dst_ref=spot(there, d, end),
             send_sem=halo_send.at[leaving.index(i)],
             recv_sem=halo_recv.at[leaving.index(i)],
@@ -421,17 +445,23 @@
 
     def stay(i):
         d, start, end, _ = pieces[i]
-        return pltpu.make_async_copy(spot(target, d, start), spot(there, d, end), stay_sem.at[staying.index(i)])
-
-    for i, piece in enumerate(pieces):
-        if any(piece[3]):
-
-            @pl.when(in_mesh(piece[3]))
-            def _(i=i):
-                halo(i).start()
-
-        else:
-            stay(i).start()
+        return pltpu.make_async_copy(spot(own_q, d, start), spot(there, d, end), stay_sem.at[staying.index(i)])
+
+    def send_targets(late):
+        for i, piece in enumerate(pieces):
+            if (piece[0] in LATE) != late:
+                continue
+            if any(piece[3]):
+
+                @pl.when(in_mesh(piece[3]))
+                def _(i=i):
+                    halo(i).start()
+
+            else:
+                stay(i).start()
+
+    load_target.wait()
+    send_targets(False)
 
     inside = {}
     for axis in range(3):
@@ -457,6 +487,45 @@
                     value = value * inside[axis, place, OFFSETS[d][axis]]
             limit = value if limit is None else jnp.where(sub % side_z == z, value, limit)
         return jnp.where(point < limit, own_w[d, y], 0.0)
+
+    for copy in loads:
+        copy.wait()
+    for y in range(side_y):
+        sent_w[y] = live_weight(FLIPPED, y)
+
+    def flip(i):
+        start, end = (
+            (own_p.at[:, FLIPPED], flip_p),
+            (own_n.at[:, FLIPPED], flip_n),
+            (sent_w, flip_w),
+        )[i]
+        return pltpu.make_async_remote_copy(
+            src_ref=start,
+            dst_ref=end,
+            send_sem=flip_send.at[i],
+            recv_sem=flip_recv.at[i],
+            device_id=beside((1, 0, 0)),
+            device_id_type=MESH,
+        )
+
+    @pl.when(at_x < count_x - 1)
+    def _():
+        for i in range(3):
+            flip(i).start()
+
+    own_q_rows = own_q.reshape(3, DIRS, side_y, rows, LANES)
+
+    def local(c, d, y):
+        return own_q_rows[c, d, y] if d == FLIPPED else own_p[c, d, y]
+
+    def ahead_of(c, d, y):
+        return flip_p[c, y] if d == FLIPPED else there_rows[c, d, y]
+
+    def normal_of(c, d, y):
+        return flip_n[c, y] if d == FLIPPED else own_n[c, d, y]
+
+    def weight_of(d, y):
+        return flip_w[y] if d == FLIPPED else live_weight(d, y)
 
     def turn(parts):
         missing = LANES - rows * len(parts)
@@ -506,17 +575,19 @@
 
         lax.fori_loop(0, LANES // step, body, 0)
 
-    acc[...] = jnp.zeros_like(acc)
-
     def here(g):
         group = GROUPS[g]
-        if g == 0:
-            for copy in loads:
-                copy.wait()
+        if FLIPPED in group:
+
+            @pl.when(at_x > 0)
+            def _():
+                for i in range(3):
+                    flip(i).wait_recv()
+
         for c in range(3):
-            turned[c, g] = turn([own_p[c, d, y] for d in group for y in range(side_y)])
-            turned[3 + c, g] = turn([own_n[c, d, y] for d in group for y in range(side_y)])
-        turned[6, g] = turn([live_weight(d, y) for d in group for y in range(side_y)])
+            turned[c, g] = turn([local(c, d, y) for d in group for y in range(side_y)])
+            turned[3 + c, g] = turn([normal_of(c, d, y) for d in group for y in range(side_y)])
+        turned[6, g] = turn([weight_of(d, y) for d in group for y in range(side_y)])
         summed(g, "here")
 
     there_rows = there.reshape(3, DIRS, side_y, rows, LANES)
@@ -542,7 +613,7 @@
                 else:
                     stay(i).wait()
         for c in range(3):
-            turned[7 + c, g] = turn([there_rows[c, d, y] for d in group for y in range(side_y)])
+            turned[7 + c, g] = turn([ahead_of(c, d, y) for d in group for y in range(side_y)])
         summed(g, "there")
         whole = [jnp.sum(acc[g, r : r + 8], axis=1) for r in range(0, SUMS, 8)]
         main = jnp.concatenate(whole[: LANES // 8], axis=0).T
@@ -590,41 +661,37 @@
 
     def along(c, step):
         other = (jnp.clip(at_x + step, 0, count_x - 1), at_y, at_z)
-        return send(c, at_x, at_y, at_z, line_send.at[c], line_recv.at[c, at_x], other)
+        return send(c, at_x, at_y, at_z, sent.at[0], line_recv.at[c, at_x], other)
 
     def along_in(c, x):
-        return send(c, x, at_y, at_z, line_send.at[c], line_recv.at[c, x], (x, at_y, at_z))
-
-    def along_sent(c):
-        x = pl.ds(0, count_x - 1)
-        return send(c, x, at_y, at_z, line_send.at[c], line_recv.at[c, 0], (at_x, at_y, at_z))
+        return send(c, x, at_y, at_z, sent.at[0], line_recv.at[c, x], (x, at_y, at_z))
 
     def across(c, x, way):
         other = (at_x, near_y[way], at_z)
-        return send(c, x, at_y, at_z, side_send.at[c, way], side_recv.at[c, way], other)
+        return send(c, x, at_y, at_z, sent.at[1], side_recv.at[c, way], other)
 
     def across_in(c, way):
         other = (at_x, near_y[way], at_z)
-        return send(c, everyone, near_y[way], at_z, side_send.at[c, way], side_recv.at[c, way], other)
+        return send(c, everyone, near_y[way], at_z, sent.at[1], side_recv.at[c, way], other)
 
     def relay(c, way):
         other = (at_x, near_y[1 - way], at_z)
-        sems = side_send.at[c, 2 + way], side_recv.at[c, 2 + way]
+        sems = sent.at[3 + way], side_recv.at[c, 2 + way]
         return send(c, halves[way], near_y[way], at_z, *sems, other)
 
     def relay_in(c, way):
         other = (at_x, near_y[1 - way], at_z)
-        sems = side_send.at[c, 2 + way], side_recv.at[c, 2 + way]
+        sems = sent.at[3 + way], side_recv.at[c, 2 + way]
         return send(c, halves[way], near_y[2], at_z, *sems, other)
 
     def core_out(c, x, y, k):
         other = (at_x, at_y, (at_z + k) % count_z)
-        return send(c, x, y, at_z, core_send.at[c, k - 1], core_recv.at[c, k - 1], other)
+        return send(c, x, y, at_z, sent.at[2], core_recv.at[c, k - 1], other)
 
     def core_all(c, z, k):
         other = (at_x, at_y, (at_z + k) % count_z)
         every_y = pl.ds(0, count_y)
-        return send(c, everyone, every_y, z, core_send.at[c, k - 1], core_recv.at[c, k - 1], other)
+        return send(c, everyone, every_y, z, sent.at[2], core_recv.at[c, k - 1], other)
 
     def to_cores(c, x, y):
         for k in range(1, count_z):
@@ -689,26 +756,37 @@
         "load": load,
     }
     for entry in SCHEDULE:
+        if entry == "late":
+            send_targets(True)
+            continue
         name, g = entry.split()
         actions[name](int(g))
 
-    for c in range(len(CHUNKS)):
-        along_sent(c).wait_send()
-        for way in range(2):
-            across_in(c, way).wait_send()
-        if c in DIRECT:
-            across_in(c, 2).wait_send()
-        else:
-            for way in range(2):
-                relay(c, way).wait_send()
-        for k in range(1, count_z):
-            core_all(c, at_z, k).wait_send()
+    def all_sent(kind, region):
+        pltpu.make_async_remote_copy(
+            src_ref=region,
+            dst_ref=region,
+            send_sem=sent.at[kind],
+            recv_sem=core_recv.at[0, 0],
+            device_id=(at_x, at_y, (at_z + 1) % count_z),
+            device_id_type=MESH,
+        ).wait_send()
+
+    assert len(DIRECT) == len(CHUNKS)
+    all_sent(0, out.at[at_z, pl.ds(0, count_x - 1), 0])
+    all_sent(1, out.at[at_z, :, pl.ds(0, 3)])
+    all_sent(2, out.at[pl.ds(0, count_z - 1)])
     for i, piece in enumerate(pieces):
         if any(piece[3]):
 
             @pl.when(in_mesh(piece[3]))
             def _(i=i):
                 halo(i).wait_send()
+
+    @pl.when(at_x < count_x - 1)
+    def _():
+        for i in range(3):
+            flip(i).wait_send()
 
     solver.run(anchor, result_out, tiles)
 
@@ -758,21 +836,26 @@
             pltpu.VMEM((36, 8, span // 2), jnp.float32),
             pltpu.VMEM((span // 2, LANES), jnp.float32),
             dma((3,)),
+            pltpu.VMEM((3, DIRS, bricks[1], chunks, bricks[2], LANES), jnp.float32),
             pltpu.VMEM((3,) + own, jnp.float32),
             pltpu.VMEM((3,) + own, jnp.float32),
             pltpu.VMEM(own, jnp.float32),
+            pltpu.VMEM(own[1:], jnp.float32),
+            pltpu.VMEM((3,) + own[1:], jnp.float32),
+            pltpu.VMEM((3,) + own[1:], jnp.float32),
+            pltpu.VMEM(own[1:], jnp.float32),
             pltpu.VMEM((3, DIRS, bricks[1], chunks, bricks[2], LANES), jnp.float32),
             pltpu.VMEM((10, len(GROUPS), LANES, LANES), jnp.float32),
             pltpu.VMEM((len(GROUPS), SUMS, 8, LANES), jnp.float32),
-            dma((3,)),
+            dma((4,)),
             dma((len(pieces) - remote,)),
             dma((remote,)),
             dma((remote,)),
-            dma((groups,)),
+            dma((3,)),
+            dma((3,)),
+            dma((3,)),
             dma((groups, devices[0])),
-            dma((groups, 4)),
-            dma((groups, 4)),
-            dma((groups, devices[2] - 1)),
+            dma((groups, 3)),
             dma((groups, devices[2] - 1)),
         ],
         compiler_params=params(collective_id=0, has_side_effects=True),

time: 37.5 us -> 35.3 us (0.941)
  Pallas kernels: 34.6 us -> 32.4 us
    pallas_call x1, Pallas kernels: 34.6 us -> 32.4 us  [on_device(): pl.pallas_call(functools.partial(step_kernel, devices, bricks), out_shape...]
where the time goes in v4:
time: 35.3 us; the launch traced here: 35.1 us
  Pallas kernels  32.4 us (92%)
  local copies, waits for them, and re-layouts  1.41 us (4%)
  between operations  1.29 us (4%)
    pallas_call x1, Pallas kernels, on_device(): pl.pallas_call(functools.partial(step_kernel, devices, bricks), out_shape...  32.4 us
    reshape x1, local copies, waits for them, and re-layouts, placed(): return jnp.transpose(value, (2, 0, 1)).reshape((12,) + bricks)  1.41 us

profile of v4, /device:TPU:0, one launch (start us, length us, event | category | flops | bytes accessed | tf_op | source)
XLA Modules:
  0.0 35.1 jit_solution(2827395304907690777)
XLA Ops:
  1.3 32.4 %step.1 = f32[4,2,24]{2,1,0:T(2,128)} custom-call(s32[1]{0:T(128)S(6)} %copy.18.anchor_in, s32[4,2,13]{2,1,0:T(2,128)} %bitcast.36, f32[4,2,12]{2,1,0:T(2,128)} %bitcast.37, f32[3,13,4,8,128]{4,3,2,1,0:T(8,128)} %bitcast.32, f32[3,13,4,4,2,128]{5,4,3,2,1,0:T(2,128)} %bitcast.33, f32[3,13,4,8,128]{4,3,2,1,0:T(8,128)} %bitcast.34, f32[13,4,8,128]{3,2,1,0:T(8,128)} %bitcast.35), custom_call_target="tpu_custom_call" | custom-call | tf_op jit(solution)/shard_map/step/pallas_call | solution.py:823
  33.7 1.4 %slice_bitcast_fusion = (f32[12,1,4,2]{0,3,2,1:T(2,128)}, f32[12,1,4,2]{0,3,2,1:T(2,128)}) fusion(f32[4,2,24]{2,1,0:T(2,128)} %step.1), kind=kLoop, calls=%fused_computation | loop fusion | bytes 1536 | tf_op jit(solution)/shard_map/reshape | solution.py:873

commit v5 on v4

--- a/solution.py
+++ b/solution.py
@@ -88,6 +88,30 @@
             for z_from, z_to, z_step in moves(dz, bricks[2]):
                 pieces.append((d, (y_from, z_from), (y_to, z_to), (-dx, y_step, z_step)))
     return pieces
+
+
+def size_of(piece):
+    _, (y, z), _, _ = piece
+    return (y.stop - y.start) * (z.stop - z.start)
+
+
+def arrivals(pieces):
+    result = {}
+    for piece in pieces:
+        if any(piece[3]):
+            key = next(g for g, group in enumerate(GROUPS) if piece[0] in group), piece[3]
+            result[key] = result.get(key, 0) + size_of(piece)
+    return result
+
+
+def box_of(size, bricks):
+    return next(
+        (a, b, c)
+        for a in range(1, DIRS + 1)
+        for b in range(1, bricks[1] + 1)
+        for c in range(1, bricks[2] + 1)
+        if a * b * c == size
+    )
 
 
 def all_of(conditions):
@@ -358,7 +382,8 @@
     at = tuple(lax.axis_index(name) for name in AXES)
     at_x, at_y, at_z = at
     pieces = halo_pieces(bricks)
-    leaving = [i for i, piece in enumerate(pieces) if any(piece[3])]
+    arrive = arrivals(pieces)
+    arrive_at = list(arrive)
     staying = [i for i, piece in enumerate(pieces) if not any(piece[3])]
     chunks = source.shape[3] // side_z
 
@@ -434,11 +459,24 @@
 
     def halo(i):
         d, start, end, step = pieces[i]
+        g = next(g for g, group in enumerate(GROUPS) if d in group)
         return pltpu.make_async_remote_copy(
             src_ref=spot(own_q, d, start),
             dst_ref=spot(there, d, end),
-            send_sem=halo_send.at[leaving.index(i)],
-            recv_sem=halo_recv.at[leaving.index(i)],
+            send_sem=halo_send.at[arrive_at.index((g, step))],
+            recv_sem=halo_recv.at[arrive_at.index((g, step))],
+            device_id=beside(step),
+            device_id_type=MESH,
+        )
+
+    def halo_bytes(size, leaves, arrives, step):
+        a, b, c = box_of(size, bricks)
+        box = (slice(None), slice(0, a), slice(0, b), slice(None), slice(0, c))
+        return pltpu.make_async_remote_copy(
+            src_ref=own_q.at[box],
+            dst_ref=there.at[box],
+            send_sem=halo_send.at[leaves],
+            recv_sem=halo_recv.at[arrives],
             device_id=beside(step),
             device_id_type=MESH,
         )
@@ -602,16 +640,16 @@
 
     def there_sums(g):
         group = GROUPS[g]
+        for place, ((of, step), size) in enumerate(arrive.items()):
+            if of == g:
+
+                @pl.when(in_mesh(tuple(-s for s in step)))
+                def _(place=place, size=size, step=step):
+                    halo_bytes(size, 0, place, step).wait_recv()
+
         for i, piece in enumerate(pieces):
-            if piece[0] in group:
-                if any(piece[3]):
-
-                    @pl.when(in_mesh(tuple(-s for s in piece[3])))
-                    def _(i=i):
-                        halo(i).wait_recv()
-
-                else:
-                    stay(i).wait()
+            if piece[0] in group and not any(piece[3]):
+                stay(i).wait()
         for c in range(3):
             turned[7 + c, g] = turn([ahead_of(c, d, y) for d in group for y in range(side_y)])
         summed(g, "there")
@@ -776,12 +814,11 @@
     all_sent(0, out.at[at_z, pl.ds(0, count_x - 1), 0])
     all_sent(1, out.at[at_z, :, pl.ds(0, 3)])
     all_sent(2, out.at[pl.ds(0, count_z - 1)])
-    for i, piece in enumerate(pieces):
-        if any(piece[3]):
-
-            @pl.when(in_mesh(piece[3]))
-            def _(i=i):
-                halo(i).wait_send()
+    for place, ((_, step), size) in enumerate(arrive.items()):
+
+        @pl.when(in_mesh(step))
+        def _(place=place, size=size, step=step):
+            halo_bytes(size, place, 0, step).wait_send()
 
     @pl.when(at_x < count_x - 1)
     def _():
@@ -849,8 +886,8 @@
             pltpu.VMEM((len(GROUPS), SUMS, 8, LANES), jnp.float32),
             dma((4,)),
             dma((len(pieces) - remote,)),
-            dma((remote,)),
-            dma((remote,)),
+            dma((len(arrivals(pieces)),)),
+            dma((len(arrivals(pieces)),)),
             dma((3,)),
             dma((3,)),
             dma((3,)),

time: 35.3 us -> 35.1 us (level)
  no operation moved by 1% of the time
where the time goes in v5:
time: 35.1 us; the launch traced here: 35 us
  Pallas kernels  32.3 us (92%)
  local copies, waits for them, and re-layouts  1.41 us (4%)
  between operations  1.29 us (4%)
    pallas_call x1, Pallas kernels, on_device(): pl.pallas_call(functools.partial(step_kernel, devices, bricks), out_shape...  32.3 us
    reshape x1, local copies, waits for them, and re-layouts, placed(): return jnp.transpose(value, (2, 0, 1)).reshape((12,) + bricks)  1.41 us

profile of v5, /device:TPU:0, one launch (start us, length us, event | category | flops | bytes accessed | tf_op | source)
XLA Modules:
  0.0 35.0 jit_solution(6134424879842952462)
XLA Ops:
  1.3 32.3 %step.1 = f32[4,2,24]{2,1,0:T(2,128)} custom-call(s32[1]{0:T(128)S(6)} %copy.18.anchor_in, s32[4,2,13]{2,1,0:T(2,128)} %bitcast.36, f32[4,2,12]{2,1,0:T(2,128)} %bitcast.37, f32[3,13,4,8,128]{4,3,2,1,0:T(8,128)} %bitcast.32, f32[3,13,4,4,2,128]{5,4,3,2,1,0:T(2,128)} %bitcast.33, f32[3,13,4,8,128]{4,3,2,1,0:T(8,128)} %bitcast.34, f32[13,4,8,128]{3,2,1,0:T(8,128)} %bitcast.35), custom_call_target="tpu_custom_call" | custom-call | tf_op jit(solution)/shard_map/step/pallas_call | solution.py:860
  33.5 1.4 %slice_bitcast_fusion = (f32[12,1,4,2]{0,3,2,1:T(2,128)}, f32[12,1,4,2]{0,3,2,1:T(2,128)}) fusion(f32[4,2,24]{2,1,0:T(2,128)} %step.1), kind=kLoop, calls=%fused_computation | loop fusion | bytes 1536 | tf_op jit(solution)/shard_map/reshape | solution.py:910
